TPU v7x, 512 devices: a whole 4x8x8 slice. The times are simulated.
512 devices in a mesh: gx: 4 (over x), gy: 8 (over z), gz: 16 (over y, core).
Axes of the slice: x: 4, y: 8, z: 8, core: 2. Of those that a mesh axis runs over, the one named last changes fastest.
Arguments:
- positions: float32 [3, 262144], P(None, ('gx', 'gy', 'gz')), may hold values from -6 to 6
- frames: float32 [128, 3, 4096], P(None, None, ('gy', 'gz')), may hold values from -6 to 6
- path_slot: int32 [512, 32], P(('gx', 'gy', 'gz')), may hold values from 0 to 511, as said below
- path_count: int32 [512], replicated, may hold values from 1 to 32, 4096 in all
- path_order: int32 [4096], replicated, may hold values from 0 to 4095, each once
- frame_rank: int32 [128], replicated, may hold values from 0 to 127, each once
Outputs:
- forces: float32 [3, 262144], P(None, ('gx', 'gy', 'gz'))
- path_cv: float32 [2], replicated
Inputs may be any that keep to these rules, and one draw needn't show every extreme that they name: `path_slot`: within one domain's row the 32 local atom indices are all different.
All inputs are finite; a program needn't handle non-finite values.
Results may differ from a plain program's by a relative error of at most 0.00013.
Values sent between devices are 32-bit elements; how exact they have to be, the bound alone decides.
No kernel may reach another device: no remote copies, remote signals or barrier semaphores. Data moves between devices by JAX's collectives and lax.ppermute only.
A program may use at most 64 MiB of HBM per device.

v0:
```python
import jax
import jax.numpy as jnp
from jax import lax
from jax.sharding import Mesh
from jax.sharding import PartitionSpec as P

P_SIZE = 4096
GX_GY_GZ = ("gx", "gy", "gz_0", "gz_1")
GY_GZ = ("gy", "gz_0", "gz_1")


STRENGTH = 20.0
S_HOME = 0.5
KAPPA_S = 0.5
KAPPA_Z = 0.05
PAIR_SCALE = 0.02
WIDTH_SQ = 4.0


def one_axis_at_a_time(array, axes):
    for axis in axes:
        array = lax.psum(array, axis)
    return array


def pair_block(block_pos, all_pos):
    diff = block_pos[:, :, None] - all_pos[:, None, :]
    dist_sq = jnp.sum(diff * diff, axis=0)
    weight = PAIR_SCALE * jnp.exp(-dist_sq / WIDTH_SQ)
    return jnp.sum(weight[None] * diff, axis=2)


def domain_forces(local):
    atoms = local.shape[1]
    rows = 256
    blocks = local.reshape(3, atoms // rows, rows).transpose(1, 0, 2)
    result = lax.map(lambda block: pair_block(block, local), blocks)
    return result.transpose(1, 0, 2).reshape(3, atoms)


def slot_ids(path_count, path_order, slots):
    offsets = jnp.cumsum(path_count) - path_count
    steps_k = jnp.arange(slots, dtype=jnp.int32)
    live = steps_k[None, :] < path_count[:, None]
    place = jnp.clip(offsets[:, None] + steps_k[None, :], 0, P_SIZE - 1)
    ids = jnp.where(live, path_order[place], -1)
    return (ids, live)


def cv_terms(dist, frame_rank):
    frames_n = dist.shape[0]
    expo = -STRENGTH * dist
    top = jnp.max(expo)
    expd = jnp.exp(expo - top)
    total = jnp.sum(expd)
    weight = expd / total
    progress_rank = frame_rank.astype(jnp.float32) / (frames_n - 1.0)
    s_value = jnp.sum(progress_rank * weight)
    z_value = -(top + jnp.log(total)) / STRENGTH
    grads = (
        KAPPA_S * P_SIZE * (s_value - S_HOME) * -STRENGTH * weight * (progress_rank - s_value)
        + KAPPA_Z * P_SIZE * z_value * weight
    )
    return (s_value, z_value, grads)


def summed_terms(partial_value, frame_rank):
    dist = one_axis_at_a_time(partial_value, GX_GY_GZ)
    return cv_terms(dist, frame_rank)


def body(positions, frames, path_slot, path_count, path_order, frame_rank):
    slots = path_slot.shape[1]
    local_slot = path_slot[0]
    ids, live = slot_ids(path_count, path_order, slots)
    path_pos = jnp.take(positions, local_slot, axis=1)
    here = lax.axis_index(GX_GY_GZ)
    my_ids = lax.dynamic_slice_in_dim(ids, here, 1, 0)[0]
    mask = lax.dynamic_slice_in_dim(live, here, 1, 0)[0].astype(jnp.float32)
    whole = lax.all_gather(frames, GY_GZ, axis=2, tiled=True)
    refs = jnp.take(whole, jnp.clip(my_ids, 0, P_SIZE - 1), axis=2)
    delta = path_pos[None] - refs
    partial_value = jnp.sum(jnp.sum(delta * delta, axis=1) * mask[None], axis=1) / P_SIZE
    s_value, z_value, grads = summed_terms(partial_value, frame_rank)
    bias = (
        -(2.0 / P_SIZE)
        * jnp.einsum("f,fcm->cm", grads, delta, precision=lax.Precision.HIGHEST)
        * mask[None]
    )
    forces = domain_forces(positions)
    forces = forces.at[:, local_slot].add(bias)
    return (forces, jnp.stack([s_value, z_value]))


def solution(mesh):
    finer = Mesh(
        mesh.devices.reshape(mesh.shape["gx"], mesh.shape["gy"], 8, 2), ("gx", "gy", "gz_0", "gz_1")
    )
    return jax.shard_map(
        body,
        mesh=finer,
        in_specs=(P(None, GX_GY_GZ), P(None, None, GY_GZ), P(GX_GY_GZ, None), P(), P(), P()),
        out_specs=(P(None, GX_GY_GZ), P()),
        check_vma=False,
    )
```

profile of v0, /device:TPU:1, one launch (start us, length us, event | category | flops | bytes accessed | tf_op | source)
XLA Modules:
  0.0 190.1 jit_solution(15374449258505947878)
XLA Ops:
  7.2 0.0 copy-start
  7.2 0.0 all-gather.2.cloned.1.call-start
  7.2 0.7 all-gather.2.cloned.1.call-update
  7.9 1.0 reduce-window.9
  8.9 0.1 slice.7
  9.0 0.1 slice_reduce_fusion
  9.1 0.8 bitcast_subtract_fusion.1
  9.9 0.1 compare_select_fusion
  10.0 0.1 reshape.176
  10.2 0.0 copy-done
  10.2 0.0 copy-start.1
  10.2 90.5 %gather_fusion.1 = s32[16384]{0:T(1024)S(1)} fusion(s32[4096]{0:T(1024)S(1)} %copy-done, s32[16384]{0:T(1024)S(1)} %broadcast_clamp_fusion), kind=kCustom, calls=%fused_computation.1 | custom fusion | bytes 196608 | tf_op jit(solution)/shard_map/gather | solution.py:46
  100.8 0.1 reshape.175
  100.9 0.0 copy-done.1
  100.9 0.1 copy.21
  101.0 0.0 copy-start.4
  101.0 0.0 copy-start.2
  101.1 1.5 while.10
  101.1 0.2 fusion.25
  101.3 0.1 exponential_multiply_fusion.2
  101.4 0.4 fusion.26
  101.8 0.2 fusion.25
  102.0 0.1 exponential_multiply_fusion.2
  102.1 0.4 fusion.26
  102.5 0.1 copy.20
  102.7 0.0 copy-done.4
  102.7 0.6 gather_fusion
  103.3 0.0 copy-done.2
  103.3 0.1 iota_compare_fusion
  103.5 0.1 select_bitcast_fusion
  103.6 0.0 copy-start.3
  103.6 10.7 %copy.22 = f32[128,3,4096]{0,1,2:T(4,128)} copy(f32[128,3,4096]{0,2,1:T(8,128)} %all-gather.2.cloned.1.call-done) | data formatting | bytes 12582912 | tf_op jit(solution)/shard_map/all_gather | solution.py:80
  114.3 4.0 %gather_fusion.2 = f32[32,128,3]{1,2,0:T(4,128)S(1)} fusion(f32[128,3,4096]{0,1,2:T(4,128)} %copy.22, s32[1024]{0:T(1024)S(1)} %pad_clamp_fusion), kind=kCustom, calls=%fused_computation.2 | custom fusion | bytes 98432 | tf_op jit(solution)/shard_map/jit(_take)/gather | solution.py:81
  118.3 0.1 multiply_reduce_fusion
  118.4 0.1 multiply_reduce_fusion.1
  118.5 9.3 %psum.28 = f32[128]{0:T(128)S(1)} all-reduce(f32[128]{0:T(128)S(1)} %broadcast_multiply_fusion), channel_id=1, replica_groups=mesh['gx'=4,'gy'=8,'gz_0'=8,'gz_1'=2] {'gx'}, use_global_device_ids=true, to_apply=%region_8.9 | all-reduce | flops 128 | bytes 1024 | tf_op jit(solution)/shard_map/psum | solution.py:22
  127.8 19.5 %psum.29 = f32[128]{0:T(128)S(1)} all-reduce(f32[128]{0:T(128)S(1)} %psum.28), channel_id=1, replica_groups=mesh['gx'=4,'gy'=8,'gz_0'=8,'gz_1'=2] {'gy'}, use_global_device_ids=true, to_apply=%region_9.10 | all-reduce | flops 128 | bytes 1024 | tf_op jit(solution)/shard_map/psum | solution.py:22
  147.3 13.8 %psum.30 = f32[128]{0:T(128)S(1)} all-reduce(f32[128]{0:T(128)S(1)} %psum.29), channel_id=1, replica_groups=mesh['gx'=4,'gy'=8,'gz_0'=8,'gz_1'=2] {'gz_0'}, use_global_device_ids=true, to_apply=%region_10.11 | all-reduce | flops 128 | bytes 1024 | tf_op jit(solution)/shard_map/psum | solution.py:22
  161.1 12.3 %psum.31 = f32[128]{0:T(128)S(1)} all-reduce(f32[128]{0:T(128)S(1)} %psum.30), channel_id=1, replica_groups=mesh['gx'=4,'gy'=8,'gz_0'=8,'gz_1'=2] {'gz_1'}, use_global_device_ids=true, to_apply=%region_11.12 | all-reduce | flops 128 | bytes 1024 | tf_op jit(solution)/shard_map/psum | solution.py:22
  173.4 0.6 multiply_reduce_fusion.3
  174.0 1.3 fusion.21
  176.6 0.0 copy-done.3
  176.6 2.0 %multiply_reduce_fusion.2 = (f32[]{:T(128)}, f32[128]{0:T(128)S(1)}) fusion(s32[128]{0:T(128)S(1)} %copy-done.3, f32[]{:T(128)} %fusion.21, f32[]{:T(128)} %multiply_reduce_fusion.3, f32[128]{0:T(128)S(1)} %psum.31), kind=kLoop, calls=%fused_computation.47 | loop fusion | flops 895 | bytes 1548 | tf_op jit(solution)/shard_map/reduce_sum | solution.py:58
  179.3 0.9 fusion.2
  180.2 0.1 copy.25
  180.3 1.0 scatter_custom_fusion
  181.3 0.7 copy.23
  182.0 1.3 pad_maximum_fusion
  (16 shorter events, 0.2 us)
Async XLA Ops:
  7.2 3.0 %copy-start = (s32[4096]{0:T(1024)S(1)}, s32[4096]{0:T(1024)}, u32[]{:S(2)}) copy-start(s32[4096]{0:T(1024)} %param.12) | copy-start | bytes 49156
  7.2 96.4 %all-gather.2.cloned.1.call-start = ((), (), s32[]{:S(2)}) async-start(), calls=%async_computation | async-start | bytes 6340608 | tf_op jit(solution)/shard_map/all_gather | solution.py:80
  10.2 90.7 %copy-start.1 = (f32[3,512]{1,0:T(4,128)S(1)}, f32[3,512]{1,0:T(4,128)}, u32[]{:S(2)}) copy-start(f32[3,512]{1,0:T(4,128)} %param.8) | copy-start | bytes 18436
  101.0 1.6 copy-start.4
  101.0 2.2 %copy-start.2 = (s32[512]{0:T(512)S(1)}, s32[512]{0:T(512)}, u32[]{:S(2)}) copy-start(s32[512]{0:T(512)} %param.11) | copy-start | bytes 6148
  103.6 73.0 %copy-start.3 = (s32[128]{0:T(128)S(1)}, s32[128]{0:T(128)}, u32[]{:S(2)}) copy-start(s32[128]{0:T(128)} %param.13) | copy-start | bytes 1540
Sparse Core Ops, SparseCore 0:
  11.2 91.8 all-gather.1
where the time goes:
time: 191 us; the launch traced here: 190 us
  local copies, waits for them, and re-layouts  107 us (56%)
  blocking collectives  54.9 us (29%)
  between operations  16.3 us (9%)
  other arithmetic  9.86 us (5%)
    gather x2, local copies, waits for them, and re-layouts, slot_ids(): ids = jnp.where(live, path_order[place], -1)  90.7 us
    psum x4, blocking collectives, one_axis_at_a_time(): array = lax.psum(array, axis)  54.9 us
    all_gather x1, local copies, waits for them, and re-layouts, body(): whole = lax.all_gather(frames, GY_GZ, axis=2, tiled=True)  10.7 us
    gather x1, local copies, waits for them, and re-layouts, body(): refs = jnp.take(whole, jnp.clip(my_ids, 0, P_SIZE - 1), axis=2)  3.99 us
  transfers between devices with their start and end apart: 1, of which 0 were waited for; matrix products, arithmetic and copies ran while one was open for 50% of the time, Pallas kernels for 0%

commit v1 on v0

v1 whole, which is shorter than its diff:
```python
import functools

import jax
import jax.numpy as jnp
from jax import lax
from jax.experimental import pallas as pl
from jax.experimental.pallas import tpu as pltpu
from jax.sharding import Mesh
from jax.sharding import PartitionSpec as P

P_SIZE = 4096
F = 128
ATOMS_LOCAL = 512
SLOTS = 32
LANES = 128
BLOCK = 32

ALL = ("gx", "gy", "gz_0", "gz_1")
HOLDERS = ("gy", "gz_0", "gz_1")
CHIPS = ("gy", "gz_0")
ROWS = ("gx", "gz_1")
N_CHIPS = 64
N_ROWS = 8
IDS = 2 * BLOCK

STRENGTH = 20.0
S_HOME = 0.5
KAPPA_S = 0.5
KAPPA_Z = 0.05
PAIR_SCALE = 0.02
WIDTH_SQ = 4.0

HIGHEST = lax.Precision.HIGHEST
F32 = jnp.float32
I32 = jnp.int32
VMEM = pl.BlockSpec(memory_space=pltpu.VMEM)


def holder_index():
    return lax.axis_index("gy") * 16 + lax.axis_index("gz_0") * 2 + lax.axis_index("gz_1")


def iota(shape, dim):
    return lax.broadcasted_iota(I32, shape, dim)


def call(kernel, out_shape, name, inputs, scratch=()):
    return pl.pallas_call(
        kernel,
        out_shape=out_shape,
        in_specs=[VMEM] * len(inputs),
        out_specs=jax.tree.map(lambda _: VMEM, out_shape),
        scratch_shapes=scratch,
        name=name,
        compiler_params=pltpu.CompilerParams(vmem_limit_bytes=8 << 20),
        cost_estimate=pl.CostEstimate(flops=2000000, bytes_accessed=100000, transcendentals=0),
    )(*inputs)


def pack_kernel(count_ref, order_ref, slot_ref, pos_ref, out_ref, ids_ref):
    here = lax.axis_index("gx") * 128 + holder_index()
    counts = count_ref[...]
    domain = iota(counts.shape, 0) * LANES + iota(counts.shape, 1)
    offset = jnp.sum(jnp.where(domain < here, counts, 0))
    mine = jnp.sum(jnp.where(domain == here, counts, 0))
    row = offset // LANES
    shift = offset - row * LANES
    first = order_ref[pl.ds(row, 1), :]
    second = order_ref[pl.ds(jnp.minimum(row + 1, P_SIZE // LANES - 1), 1), :]
    lane = iota((1, LANES), 1)
    k = lane & (SLOTS - 1)
    turn = jnp.where(shift == 0, 0, LANES - shift)
    ids = jnp.where(lane < LANES - shift, pltpu.roll(first, turn, 1), pltpu.roll(second, turn, 1))
    ids = jnp.where(lane < SLOTS, ids, 0)
    slots = jnp.concatenate([slot_ref[...]] * 4, axis=1)
    ids = ids + pltpu.roll(ids, 2 * SLOTS, 1)
    ids = ids + pltpu.roll(ids, SLOTS, 1)
    live = k < mine
    ids = jnp.where(live, ids, -1)
    ids_ref[...] = ids
    pick = (iota((ATOMS_LOCAL, LANES), 0) == slots).astype(F32)
    xyz = jnp.dot(pos_ref[...], pick, precision=HIGHEST, preferred_element_type=F32)
    part = lane // SLOTS
    row_out = jnp.where(part == 0, xyz[0:1], jnp.where(part == 1, xyz[1:2], xyz[2:3]))
    row_out = jnp.where(live, row_out, 0.0)
    row_out = jnp.where(part == 3, ids.astype(F32), row_out)
    out_ref[...] = jnp.broadcast_to(row_out, out_ref.shape)


def dist_kernel(got_ref, mine_ref, other_ref, out_ref, coded):
    holder = holder_index()
    chip, core = holder // 2, holder & 1
    got = got_ref[...]
    lane = iota(got.shape, 1)
    part = lane // SLOTS
    ids = jnp.where(part == 3, got, 0.0)
    ids = ids + pltpu.roll(ids, 2 * SLOTS, 1)
    ids = ids + pltpu.roll(ids, SLOTS, 1)
    coded[0] = ids
    coded[1] = jnp.where(part == 3, 1.0, got)
    j = iota((IDS, LANES), 0)
    own = (chip * IDS + (j ^ (core * BLOCK))).astype(F32)
    found = jnp.zeros((IDS, LANES), F32)
    for m in range(N_CHIPS):
        found = found + jnp.where(coded[0, m : m + 1, :] == own, coded[1, m : m + 1, :], 0.0)
    part = iota((IDS, LANES), 1) // SLOTS
    column = [jnp.sum(jnp.where(part == c, found, 0.0), axis=1, keepdims=True) for c in range(4)]
    total = jnp.zeros((BLOCK, F), F32)
    for half, frames in ((0, mine_ref), (1, other_ref)):
        low = half * BLOCK
        square = jnp.zeros((BLOCK, F), F32)
        for c in range(3):
            delta = column[c][low : low + BLOCK] - frames[c * BLOCK : (c + 1) * BLOCK, :]
            square = square + delta * delta
        total = total + square * column[3][low : low + BLOCK]
    partial = jnp.sum(total, axis=0, keepdims=True) * (1.0 / P_SIZE)
    out_ref[...] = jnp.broadcast_to(partial, out_ref.shape)


def sum_kernel(got_ref, out_ref):
    out_ref[...] = jnp.broadcast_to(jnp.sum(got_ref[...], axis=0, keepdims=True), out_ref.shape)


def bias_kernel(got_ref, rank_ref, mine_ref, other_ref, out_ref, cv_ref):
    dist = jnp.sum(got_ref[...], axis=0, keepdims=True)
    expo = -STRENGTH * dist
    top = jnp.max(expo, axis=1, keepdims=True)
    expd = jnp.exp(expo - top)
    total = jnp.sum(expd, axis=1, keepdims=True)
    weight = expd / total
    rank = rank_ref[...].astype(F32) / (F - 1.0)
    s_value = jnp.sum(rank * weight, axis=1, keepdims=True)
    z_value = -(top + jnp.log(total)) / STRENGTH
    grads = (
        KAPPA_S * P_SIZE * (s_value - S_HOME) * -STRENGTH * weight * (rank - s_value)
        + KAPPA_Z * P_SIZE * z_value * weight
    )
    lane = iota((1, LANES), 1)
    cv_ref[...] = jnp.where(lane == 0, s_value, z_value)
    eight = jnp.broadcast_to(grads, (8, F))
    dims = (((1,), (1,)), ((), ()))
    own = lax.dot_general(eight, mine_ref[...], dims, precision=HIGHEST, preferred_element_type=F32)
    oth = lax.dot_general(eight, other_ref[...], dims, precision=HIGHEST, preferred_element_type=F32)
    whole = jnp.broadcast_to(jnp.sum(grads, axis=1, keepdims=True), (1, BLOCK))
    own = jnp.concatenate([own[0:1], whole], axis=1)
    oth = jnp.concatenate([oth[0:1], whole], axis=1)
    out_ref[...] = jnp.where((iota(out_ref.shape, 0) & 1) == 0, own, oth)


def pair_kernel(pos_ref, out_ref):
    pos = pos_ref[...]
    columns = jnp.transpose(jnp.concatenate([pos, pos[0:1]] * 2, axis=0))
    scale = -1.0 / (WIDTH_SQ * 0.6931471805599453)
    step = 64
    sums = [jnp.zeros((8, ATOMS_LOCAL), F32) for _ in range(3)]
    for i in range(0, ATOMS_LOCAL, step):
        diff = [pos[c : c + 1, :] - columns[i : i + step, c : c + 1] for c in range(3)]
        dist_sq = diff[0] * diff[0] + diff[1] * diff[1] + diff[2] * diff[2]
        weight = jnp.exp2(dist_sq * scale)
        for c in range(3):
            term = weight * diff[c]
            for r in range(0, step, 8):
                sums[c] = sums[c] + term[r : r + 8]
    for c in range(3):
        out_ref[c : c + 1, :] = PAIR_SCALE * jnp.sum(sums[c], axis=0, keepdims=True)


def force_kernel(got_ref, ids_ref, slot_ref, pos_ref, pair_ref, out_ref):
    core = lax.axis_index("gz_1")
    ids = ids_ref[:, 0:SLOTS]
    source = (ids // BLOCK) ^ core
    from_row = (iota((2 * N_CHIPS, SLOTS), 0) == source).astype(F32)
    dims = (((0,), (0,)), ((), ()))
    rows = lax.dot_general(got_ref[...], from_row, dims, precision=HIGHEST, preferred_element_type=F32)
    at = (iota((BLOCK, SLOTS), 0) == (ids & (BLOCK - 1))).astype(F32)
    slots = slot_ref[...]
    pick = (iota((ATOMS_LOCAL, SLOTS), 0) == slots).astype(F32)
    sums = [jnp.sum(rows[c * BLOCK : (c + 1) * BLOCK] * at, axis=0, keepdims=True) for c in range(3)]
    whole = rows[96:97]
    live = (ids >= 0).astype(F32)
    scattered = lax.dot_general(
        jnp.concatenate(sums + [whole] * 5, axis=0) * live,
        pick,
        (((1,), (1,)), ((), ())),
        precision=HIGHEST,
        preferred_element_type=F32,
    )
    bias = (-2.0 / P_SIZE) * (pos_ref[...] * scattered[3:4] - scattered[0:3])
    out_ref[...] = pair_ref[...] + bias


def shaped(*shape, dtype=F32):
    return jax.ShapeDtypeStruct(shape, dtype)


def spread(rows, axes):
    return lax.all_to_all(rows, axes, 0, 0, tiled=True)


def body(positions, frames, path_slot, path_count, path_order, frame_rank):
    mine = jnp.transpose(frames, (1, 2, 0)).reshape(3 * BLOCK, F)
    other = lax.ppermute(mine, "gz_1", [(0, 1), (1, 0)])
    sent, ids = call(
        pack_kernel,
        (shaped(N_CHIPS, LANES), shaped(1, LANES, dtype=I32)),
        "pack",
        (path_count.reshape(4, LANES), path_order.reshape(32, LANES), path_slot, positions),
    )
    pair = call(pair_kernel, shaped(3, ATOMS_LOCAL), "pair", (positions,))
    atoms = spread(sent, CHIPS)
    coded = [pltpu.VMEM((2, N_CHIPS, LANES), F32)]
    partial = call(dist_kernel, shaped(N_CHIPS, LANES), "dist", (atoms, mine, other), coded)
    over_chips = spread(partial, CHIPS)
    row_sum = call(sum_kernel, shaped(N_ROWS, LANES), "sum", (over_chips,))
    over_rows = spread(row_sum, ROWS)
    biases, cv = call(
        bias_kernel,
        (shaped(2 * N_CHIPS, LANES), shaped(1, LANES)),
        "bias",
        (over_rows, frame_rank.reshape(1, F), mine, other),
    )
    back = spread(biases, CHIPS)
    forces = call(
        force_kernel, shaped(3, ATOMS_LOCAL), "force", (back, ids, path_slot, positions, pair)
    )
    return forces, cv[0, 0:2]


def solution(mesh):
    finer = Mesh(mesh.devices.reshape(mesh.shape["gx"], mesh.shape["gy"], 8, 2), ALL)
    return jax.shard_map(
        body,
        mesh=finer,
        in_specs=(P(None, ALL), P(None, None, HOLDERS), P(ALL, None), P(), P(), P()),
        out_specs=(P(None, ALL), P()),
        check_vma=False,
    )
```

time: 191 us -> 78.9 us (0.41)
  local copies, waits for them, and re-layouts: 107 us -> 3.26 us
  blocking collectives: 54.9 us -> 16 us
  starting transfers between devices: 0.04 us -> 31 us
  waiting for transfers between devices: 0.68 us -> 22.3 us
  between operations: 16.3 us -> 0.7 us
  other arithmetic: 9.86 us -> 0 us
  Pallas kernels: 0 us -> 5.18 us
    gather x4 -> x0, local copies, waits for them, and re-layouts: 95.2 us -> none  [the longest x2 90.7 us: slot_ids(): ids = jnp.where(live, path_order[place], -1)]
    psum x4 -> x0, blocking collectives: 54.9 us -> none  [one_axis_at_a_time(): array = lax.psum(array, axis)]
    all_to_all x0 -> x3, starting transfers between devices: none -> 28.1 us  [spread(): return lax.all_to_all(rows, axes, 0, 0, tiled=True)]
    all_to_all x0 -> x3, waiting for transfers between devices: none -> 21.4 us  [spread(): return lax.all_to_all(rows, axes, 0, 0, tiled=True)]
    all_to_all x0 -> x1, blocking collectives: none -> 16 us  [spread(): return lax.all_to_all(rows, axes, 0, 0, tiled=True)]
    all_gather x1 -> x0, local copies, waits for them, and re-layouts: 10.7 us -> none  [body(): whole = lax.all_gather(frames, GY_GZ, axis=2, tiled=True)]
    pallas_call x0 -> x6, Pallas kernels: none -> 5.18 us  [call(): pl.pallas_call(kernel, out_shape=out_shape, in_specs=[VMEM] * len(inputs)...]
    reduce_sum x8 -> x0, other arithmetic: 4.64 us -> none  [the longest x1 1.98 us: cv_terms(): s_value = jnp.sum(progress_rank * weight)]
  transfers between devices with their start and end apart: 1 -> 4, of which waited for: 0 -> 4; matrix products, arithmetic and copies ran while one was open for 50% -> 1% of each run, Pallas kernels for 0% -> 1%
where the time goes in v1:
time: 78.9 us; the launch traced here: 78.4 us
  starting transfers between devices  31 us (39%)
  waiting for transfers between devices  22.3 us (28%)
  blocking collectives  16 us (20%)
  Pallas kernels  5.18 us (7%)
  local copies, waits for them, and re-layouts  3.26 us (4%)
    all_to_all x3, starting transfers between devices, spread(): return lax.all_to_all(rows, axes, 0, 0, tiled=True)  28.1 us
    all_to_all x3, waiting for transfers between devices, spread(): return lax.all_to_all(rows, axes, 0, 0, tiled=True)  21.4 us
    all_to_all x1, blocking collectives, spread(): return lax.all_to_all(rows, axes, 0, 0, tiled=True)  16 us
    pallas_call x6, Pallas kernels, call(): pl.pallas_call(kernel, out_shape=out_shape, in_specs=[VMEM] * len(inputs)...  5.18 us
    ppermute x1, starting transfers between devices, body(): other = lax.ppermute(mine, 'gz_1', [(0, 1), (1, 0)])  2.86 us
    unnamed x14, local copies, waits for them, and re-layouts  2.75 us
  transfers between devices with their start and end apart: 4, of which 4 were waited for; matrix products, arithmetic and copies ran while one was open for 1% of the time, Pallas kernels for 1%

profile of v1, /device:TPU:1, one launch (start us, length us, event | category | flops | bytes accessed | tf_op | source)
XLA Modules:
  0.0 78.4 jit_solution(8961326135283751448)
XLA Ops:
  0.6 0.0 copy-start.5
  0.6 0.0 copy-start.4
  0.7 0.7 copy-done.5
  1.3 0.0 copy-done.4
  1.3 0.0 copy-start.1
  1.3 0.7 copy-done.1
  2.0 0.0 copy-start.3
  2.0 0.7 copy-done.3
  2.7 0.0 copy-start
  2.7 1.0 %pack.1 = (f32[64,128]{1,0:T(8,128)}, s32[1,128]{1,0:T(1,128)S(1)}) custom-call(s32[4,128]{1,0:T(4,128)S(1)} %bitcast.31, s32[32,128]{1,0:T(8,128)S(1)} %bitcast.30, s32[1,32]{1,0:T(1,128)S(1)} %copy-done.4, f32[3,512]{1,0:T(4,128)S(1)} %copy-done.1), custom_call_target="tpu_custom_call" | custom-call | flops 2000000 | bytes 100000 | tf_op jit(solution)/shard_map/pack/pallas_call | solution.py:48
  3.7 17.1 %all-to-all-start = ((f32[64,1,128]{2,1,0:T(1,128)}), f32[64,1,128]{2,1,0:T(1,128)S(1)}, u32[]{:S(2)}, u32[]{:S(2)}) async-start(f32[64,1,128]{2,1,0:T(1,128)} %bitcast.3), calls=%async_computation | async-start | bytes 65536 | tf_op jit(solution)/shard_map/all_to_all | solution.py:197
  20.8 0.0 copy-done
  20.8 2.9 %collective-permute-start = (f32[96,128]{1,0:T(8,128)S(1)}, f32[96,128]{1,0:T(8,128)S(1)}, u32[]{:S(2)}, u32[]{:S(2)}) collective-permute-start(f32[96,128]{1,0:T(8,128)S(1)} %bitcast.23), channel_id=1, source_target_pairs={{0,1},{1,0},{2,3},{3,2},{4,5},{5,4},{6,7},{7,6},{8,9},{9,8},{10,11... | collective-permute-start | bytes 147464 | tf_op jit(solution)/shard_map/ppermute | solution.py:202
  23.7 0.9 %collective-permute-done.other_ref = f32[96,128]{1,0:T(8,128)S(1)} collective-permute-done((f32[96,128]{1,0:T(8,128)S(1)}, f32[96,128]{1,0:T(8,128)S(1)}, u32[]{:S(2)}, u32[]{:S(2)}) %collective-permute-start) | collective-permute-done | bytes 49184 | tf_op jit(solution)/shard_map/ppermute | solution.py:202
  24.6 7.1 %all-to-all-done = f32[64,1,128]{2,1,0:T(1,128)S(1)} async-done(((f32[64,1,128]{2,1,0:T(1,128)}), f32[64,1,128]{2,1,0:T(1,128)S(1)}, u32[]{:S(2)}, u32[]{:S(2)}) %all-to-all-start) | async-done | bytes 32800 | tf_op jit(solution)/shard_map/all_to_all | solution.py:197
  31.7 0.5 dist.1
  32.2 16.0 %all_to_all.44 = f32[64,1,128]{2,1,0:T(1,128)S(1)} all-to-all(f32[64,1,128]{2,1,0:T(1,128)S(1)} %bitcast.27), channel_id=1, replica_groups=mesh['gx'=4,'gy'=8,'gz_0'=8,'gz_1'=2] {'gy','gz_0'}, dimensions={0} | all-to-all | bytes 65536 | tf_op jit(solution)/shard_map/all_to_all | solution.py:197
  48.1 0.6 sum.1
  48.8 0.0 copy-start.2
  48.8 6.4 %all-to-all-start.2 = ((f32[8,1,128]{2,1,0:T(1,128)}), f32[8,1,128]{2,1,0:T(1,128)S(1)}, u32[]{:S(2)}, u32[]{:S(2)}) async-start(f32[8,1,128]{2,1,0:T(1,128)} %bitcast.12), calls=%async_computation.2 | async-start | bytes 8192 | tf_op jit(solution)/shard_map/all_to_all | solution.py:197
  55.2 0.0 copy-done.2
  55.2 0.8 %pair.1.pair_ref = f32[3,512]{1,0:T(4,128)S(1)} custom-call(f32[3,512]{1,0:T(4,128)S(1)} %copy-done.2), custom_call_target="tpu_custom_call" | custom-call | flops 2000000 | bytes 100000 | tf_op jit(solution)/shard_map/pair/pallas_call | solution.py:48
  56.0 3.7 %all-to-all-done.2 = f32[8,1,128]{2,1,0:T(1,128)S(1)} async-done(((f32[8,1,128]{2,1,0:T(1,128)}), f32[8,1,128]{2,1,0:T(1,128)S(1)}, u32[]{:S(2)}, u32[]{:S(2)}) %all-to-all-start.2) | async-done | bytes 4128 | tf_op jit(solution)/shard_map/all_to_all | solution.py:197
  59.7 0.0 copy-start.6
  59.7 0.7 copy-done.6
  60.3 1.1 %bias.1 = (f32[128,128]{1,0:T(8,128)}, f32[1,128]{1,0:T(1,128)S(1)}) custom-call(f32[8,128]{1,0:T(8,128)S(1)} %bitcast.29, s32[1,128]{1,0:T(1,128)S(1)} %bitcast.32, f32[96,128]{1,0:T(8,128)S(1)} %bitcast.25, f32[96,128]{1,0:T(8,128)S(1)} %collective-permute-done.other_ref), custom_call_target="tpu_custom_call" | custom-call | flops 2000000 | bytes 100000 | tf_op jit(solution)/shard_map/bias/pallas_call | solution.py:48
  61.5 4.6 %all-to-all-start.3 = ((f32[64,2,128]{2,1,0:T(2,128)}), f32[64,2,128]{2,1,0:T(2,128)S(1)}, u32[]{:S(2)}, u32[]{:S(2)}) async-start(f32[64,2,128]{2,1,0:T(2,128)} %bitcast.15), calls=%async_computation.3 | async-start | bytes 131072 | tf_op jit(solution)/shard_map/all_to_all | solution.py:197
  66.1 0.5 slice_bitcast_fusion
  66.6 10.6 %all-to-all-done.3 = f32[64,2,128]{2,1,0:T(2,128)S(1)} async-done(((f32[64,2,128]{2,1,0:T(2,128)}), f32[64,2,128]{2,1,0:T(2,128)S(1)}, u32[]{:S(2)}, u32[]{:S(2)}) %all-to-all-start.3) | async-done | bytes 65568 | tf_op jit(solution)/shard_map/all_to_all | solution.py:197
  77.2 1.2 %force.1 = f32[3,512]{1,0:T(4,128)} custom-call(f32[128,128]{1,0:T(8,128)S(1)} %bitcast.22, s32[1,128]{1,0:T(1,128)S(1)} %get-tuple-element.8.ids_ref, s32[1,32]{1,0:T(1,128)S(1)} %copy-done.4, f32[3,512]{1,0:T(4,128)S(1)} %copy-done.2, f32[3,512]{1,0:T(4,128)S(1)} %pair.1.pair_ref), custom_call_target="tpu_custom_call" | custom-call | flops 2000000 | bytes 100000 | tf_op jit(solution)/shard_map/force/pallas_call | solution.py:48
Async XLA Ops:
  0.6 0.7 copy-start.5
  0.6 0.7 copy-start.4
  1.3 0.7 copy-start.1
  2.0 0.7 copy-start.3
  2.7 18.1 %copy-start = (f32[128,3,32]{0,2,1:T(8,128)S(1)}, f32[128,3,32]{0,2,1:T(8,128)}, u32[]{:S(2)}) copy-start(f32[128,3,32]{0,2,1:T(8,128)} %param.7) | copy-start | bytes 147460
  3.7 28.0 %all-to-all-start = ((f32[64,1,128]{2,1,0:T(1,128)}), f32[64,1,128]{2,1,0:T(1,128)S(1)}, u32[]{:S(2)}, u32[]{:S(2)}) async-start(f32[64,1,128]{2,1,0:T(1,128)} %bitcast.3), calls=%async_computation | async-start | bytes 65536 | tf_op jit(solution)/shard_map/all_to_all | solution.py:197
  20.8 3.7 %collective-permute-start = (f32[96,128]{1,0:T(8,128)S(1)}, f32[96,128]{1,0:T(8,128)S(1)}, u32[]{:S(2)}, u32[]{:S(2)}) collective-permute-start(f32[96,128]{1,0:T(8,128)S(1)} %bitcast.23), channel_id=1, source_target_pairs={{0,1},{1,0},{2,3},{3,2},{4,5},{5,4},{6,7},{7,6},{8,9},{9,8},{10,11... | collective-permute-start | bytes 147464 | tf_op jit(solution)/shard_map/ppermute | solution.py:202
  48.8 6.4 %copy-start.2 = (f32[3,512]{1,0:T(4,128)S(1)}, f32[3,512]{1,0:T(4,128)}, u32[]{:S(2)}) copy-start(f32[3,512]{1,0:T(4,128)} %pos_ref.5) | copy-start | bytes 18436
  48.8 10.9 %all-to-all-start.2 = ((f32[8,1,128]{2,1,0:T(1,128)}), f32[8,1,128]{2,1,0:T(1,128)S(1)}, u32[]{:S(2)}, u32[]{:S(2)}) async-start(f32[8,1,128]{2,1,0:T(1,128)} %bitcast.12), calls=%async_computation.2 | async-start | bytes 8192 | tf_op jit(solution)/shard_map/all_to_all | solution.py:197
  59.7 0.7 copy-start.6
  61.5 15.7 %all-to-all-start.3 = ((f32[64,2,128]{2,1,0:T(2,128)}), f32[64,2,128]{2,1,0:T(2,128)S(1)}, u32[]{:S(2)}, u32[]{:S(2)}) async-start(f32[64,2,128]{2,1,0:T(2,128)} %bitcast.15), calls=%async_computation.3 | async-start | bytes 131072 | tf_op jit(solution)/shard_map/all_to_all | solution.py:197

commit v2 on v0

v2 whole, which is shorter than its diff:
```python
import math

import jax
import jax.numpy as jnp
from jax import lax
from jax.experimental import pallas as pl
from jax.experimental.pallas import tpu as pltpu
from jax.sharding import Mesh
from jax.sharding import PartitionSpec as P

P_SIZE = 4096
F = 128
ATOMS_LOCAL = 512
SLOTS = 32
LANES = 128
BLOCK = 32

ALL = ("gx", "gy", "gz_0", "gz_1")
HOLDERS = ("gy", "gz_0", "gz_1")
N_HOLDERS = 128
FIRST = ("gx", "gy")
N_FIRST = 32
SECOND = ("gz_0", "gz_1")
N_SECOND = 16

STRENGTH = 20.0
S_HOME = 0.5
KAPPA_S = 0.5
KAPPA_Z = 0.05
PAIR_SCALE = 0.02
WIDTH_SQ = 4.0

HIGHEST = lax.Precision.HIGHEST
F32 = jnp.float32
I32 = jnp.int32
VMEM = pl.BlockSpec(memory_space=pltpu.VMEM)
HBM = pl.BlockSpec(memory_space=pltpu.HBM)


def holder_index():
    return lax.axis_index("gy") * 16 + lax.axis_index("gz_0") * 2 + lax.axis_index("gz_1")


def iota(shape, dim):
    return lax.broadcasted_iota(I32, shape, dim)


def shaped(*shape, dtype=F32):
    return jax.ShapeDtypeStruct(shape, dtype)


def call(kernel, out_shape, name, inputs, **kwargs):
    return pl.pallas_call(
        kernel,
        out_shape=out_shape,
        out_specs=jax.tree.map(lambda _: VMEM, out_shape),
        name=name,
        cost_estimate=pl.CostEstimate(flops=2000000, bytes_accessed=100000, transcendentals=0),
        **kwargs,
    )(*inputs)


def small(kernel, out_shape, name, inputs, scratch=()):
    return call(
        kernel,
        out_shape,
        name,
        inputs,
        in_specs=[VMEM] * len(inputs),
        scratch_shapes=scratch,
        compiler_params=pltpu.CompilerParams(vmem_limit_bytes=8 << 20),
    )


def pair_forces(pos, out_ref):
    columns = jnp.transpose(jnp.concatenate([pos, pos[0:1]] * 2, axis=0))
    scale = -1.0 / (WIDTH_SQ * math.log(2.0))
    step = 64
    sums = [jnp.zeros((8, ATOMS_LOCAL), F32) for _ in range(3)]
    for i in range(0, ATOMS_LOCAL, step):
        diff = [pos[c : c + 1, :] - columns[i : i + step, c : c + 1] for c in range(3)]
        dist_sq = diff[0] * diff[0] + diff[1] * diff[1] + diff[2] * diff[2]
        weight = jnp.exp2(dist_sq * scale)
        for c in range(3):
            term = weight * diff[c]
            for r in range(0, step, 8):
                sums[c] = sums[c] + term[r : r + 8]
    for c in range(3):
        out_ref[c : c + 1, :] = PAIR_SCALE * jnp.sum(sums[c], axis=0, keepdims=True)


def pack_kernel(
    count_hbm, order_hbm, slot_hbm, pos_hbm, rank_hbm, out_ref, aux_ref, xyz_ref, pair_ref, count_ref, order_ref, slot_ref, pos_ref, rank_ref, sems
):
    copies = [
        pltpu.make_async_copy(source, target, sems.at[i])
        for i, (source, target) in enumerate(
            (
                (count_hbm, count_ref),
                (order_hbm, order_ref),
                (slot_hbm, slot_ref),
                (pos_hbm, pos_ref),
                (rank_hbm, rank_ref),
            )
        )
    ]
    for copy in copies:
        copy.start()
    here = lax.axis_index("gx") * N_HOLDERS + holder_index()
    copies[0].wait()
    counts = count_ref[...]
    domain = iota(counts.shape, 0) * LANES + iota(counts.shape, 1)
    offset = jnp.sum(jnp.where(domain < here, counts, 0))
    mine = jnp.sum(jnp.where(domain == here, counts, 0))
    copies[1].wait()
    row = offset // LANES
    shift = offset - row * LANES
    first = order_ref[pl.ds(row, 1), :]
    second = order_ref[pl.ds(jnp.minimum(row + 1, P_SIZE // LANES - 1), 1), :]
    lane = iota((1, LANES), 1)
    k = lane & (SLOTS - 1)
    turn = jnp.where(shift == 0, 0, LANES - shift)
    ids = jnp.where(lane < LANES - shift, pltpu.roll(first, turn, 1), pltpu.roll(second, turn, 1))
    ids = jnp.where(lane < SLOTS, ids, 0)
    copies[2].wait()
    slots = jnp.concatenate([slot_ref[...]] * 4, axis=1)
    ids = ids + pltpu.roll(ids, 2 * SLOTS, 1)
    ids = ids + pltpu.roll(ids, SLOTS, 1)
    live = k < mine
    ids = jnp.where(live, ids, -1)
    pick = (iota((ATOMS_LOCAL, LANES), 0) == slots).astype(F32)
    copies[3].wait()
    pos = pos_ref[...]
    xyz = jnp.dot(pos, pick, precision=HIGHEST, preferred_element_type=F32)
    xyz_ref[...] = xyz
    part = lane // SLOTS
    row_out = jnp.where(part == 0, xyz[0:1], jnp.where(part == 1, xyz[1:2], xyz[2:3]))
    row_out = jnp.where(live, row_out, 0.0)
    row_out = jnp.where(part == 3, ids.astype(F32), row_out)
    out_ref[...] = jnp.broadcast_to(row_out, out_ref.shape)
    copies[4].wait()
    aux_ref[...] = jnp.concatenate([ids, slots, rank_ref[...]], axis=0)
    pair_forces(pos, pair_ref)


def dist_kernel(got_ref, frames_ref, out_ref, coded):
    got = got_ref[...]
    part = iota(got.shape, 1) // SLOTS
    ids = jnp.where(part == 3, got, 0.0)
    ids = ids + pltpu.roll(ids, 2 * SLOTS, 1)
    ids = ids + pltpu.roll(ids, SLOTS, 1)
    coded[0] = ids
    coded[1] = jnp.where(part == 3, 1.0, got)
    own = (holder_index() * BLOCK + iota((BLOCK, LANES), 0)).astype(F32)
    found = [jnp.zeros((BLOCK, LANES), F32) for _ in range(2)]
    for m in range(N_HOLDERS):
        hit = jnp.where(coded[0, m : m + 1, :] == own, coded[1, m : m + 1, :], 0.0)
        found[m % 2] = found[m % 2] + hit
    found = found[0] + found[1]
    part = iota((BLOCK, LANES), 1) // SLOTS
    column = [jnp.sum(jnp.where(part == c, found, 0.0), axis=1, keepdims=True) for c in range(4)]
    square = jnp.zeros((BLOCK, F), F32)
    for c in range(3):
        delta = column[c] - frames_ref[c * BLOCK : (c + 1) * BLOCK, :]
        square = square + delta * delta
    partial = jnp.sum(square * column[3], axis=0, keepdims=True) * (1.0 / P_SIZE)
    out_ref[...] = jnp.broadcast_to(partial, out_ref.shape)


def sum_kernel(got_ref, out_ref):
    out_ref[...] = jnp.broadcast_to(jnp.sum(got_ref[...], axis=0, keepdims=True), out_ref.shape)


def bias_kernel(got_ref, aux_ref, frames_ref, out_ref, cv_ref):
    dist = jnp.sum(got_ref[...], axis=0, keepdims=True)
    expo = -STRENGTH * dist
    top = jnp.max(expo, axis=1, keepdims=True)
    expd = jnp.exp(expo - top)
    total = jnp.sum(expd, axis=1, keepdims=True)
    weight = expd / total
    rank = aux_ref[2:3, :].astype(F32) / (F - 1.0)
    s_value = jnp.sum(rank * weight, axis=1, keepdims=True)
    z_value = -(top + jnp.log(total)) / STRENGTH
    grads = (
        KAPPA_S * P_SIZE * (s_value - S_HOME) * -STRENGTH * weight * (rank - s_value)
        + KAPPA_Z * P_SIZE * z_value * weight
    )
    lane = iota((1, LANES), 1)
    cv_ref[...] = jnp.where(lane == 0, s_value, z_value)
    eight = jnp.broadcast_to(grads, (8, F))
    dims = (((1,), (1,)), ((), ()))
    own = lax.dot_general(eight, frames_ref[...], dims, precision=HIGHEST, preferred_element_type=F32)
    whole = jnp.broadcast_to(jnp.sum(grads, axis=1, keepdims=True), (1, BLOCK))
    row = jnp.concatenate([own[0:1], whole], axis=1)
    out_ref[...] = jnp.broadcast_to(row, out_ref.shape)


def force_kernel(got_ref, aux_ref, xyz_ref, pair_ref, cv_in_ref, out_ref, cv_ref):
    cv_ref[...] = cv_in_ref[:, 0:2]
    ids = aux_ref[0:1, 0:SLOTS]
    slots = aux_ref[1:2, 0:SLOTS]
    from_row = (iota((N_HOLDERS, SLOTS), 0) == ids // BLOCK).astype(F32)
    dims = (((0,), (0,)), ((), ()))
    rows = lax.dot_general(got_ref[...], from_row, dims, precision=HIGHEST, preferred_element_type=F32)
    at = (iota((BLOCK, SLOTS), 0) == (ids & (BLOCK - 1))).astype(F32)
    whole = rows[96:97]
    bias = []
    for c in range(3):
        weighted = jnp.sum(rows[c * BLOCK : (c + 1) * BLOCK] * at, axis=0, keepdims=True)
        bias.append(xyz_ref[c : c + 1, 0:SLOTS] * whole - weighted)
    live = (ids >= 0).astype(F32)
    bias = jnp.concatenate(bias + bias[0:1] * 5, axis=0) * (live * (-2.0 / P_SIZE))
    pick = (iota((ATOMS_LOCAL, SLOTS), 0) == slots).astype(F32)
    dims = (((1,), (1,)), ((), ()))
    scattered = lax.dot_general(bias, pick, dims, precision=HIGHEST, preferred_element_type=F32)
    out_ref[...] = pair_ref[...] + scattered[0:3]


def spread(rows, axes):
    return lax.all_to_all(rows, axes, 0, 0, tiled=True)


def body(positions, frames, path_slot, path_count, path_order, frame_rank):
    frames = jnp.transpose(frames, (1, 2, 0)).reshape(3 * BLOCK, F)
    inputs = (
        path_count.reshape(4, LANES),
        path_order.reshape(32, LANES),
        path_slot,
        positions,
        frame_rank.reshape(1, F),
    )
    inputs = tuple(pltpu.with_memory_space_constraint(a, pltpu.HBM) for a in inputs)
    sent, aux, xyz, pair = call(
        pack_kernel,
        (
            shaped(N_HOLDERS, LANES),
            shaped(3, LANES, dtype=I32),
            shaped(3, LANES),
            shaped(3, ATOMS_LOCAL),
        ),
        "pack",
        inputs,
        in_specs=[HBM] * len(inputs),
        scratch_shapes=[pltpu.VMEM(a.shape, a.dtype) for a in inputs]
        + [pltpu.SemaphoreType.DMA((len(inputs),))],
        compiler_params=pltpu.CompilerParams(vmem_limit_bytes=8 << 20),
    )
    atoms = spread(sent, HOLDERS)
    coded = [pltpu.VMEM((2, N_HOLDERS, LANES), F32)]
    partial = small(dist_kernel, shaped(N_FIRST, LANES), "dist", (atoms, frames), coded)
    first = spread(partial, FIRST)
    row_sum = small(sum_kernel, shaped(N_SECOND, LANES), "sum", (first,))
    second = spread(row_sum, SECOND)
    biases, cv = small(
        bias_kernel, (shaped(N_HOLDERS, LANES), shaped(1, LANES)), "bias", (second, aux, frames)
    )
    back = spread(biases, HOLDERS)
    forces, cv = small(
        force_kernel, (shaped(3, ATOMS_LOCAL), shaped(1, 2)), "force", (back, aux, xyz, pair, cv)
    )
    return forces, cv.reshape(2)


def solution(mesh):
    finer = Mesh(mesh.devices.reshape(mesh.shape["gx"], mesh.shape["gy"], 8, 2), ALL)
    return jax.shard_map(
        body,
        mesh=finer,
        in_specs=(P(None, ALL), P(None, None, HOLDERS), P(ALL, None), P(), P(), P()),
        out_specs=(P(None, ALL), P()),
        check_vma=False,
    )
```

time: 191 us -> 77 us (0.40)
  local copies, waits for them, and re-layouts: 107 us -> 0.01 us
  blocking collectives: 54.9 us -> 71.8 us
  between operations: 16.3 us -> 0.66 us
  other arithmetic: 9.86 us -> 0 us
  Pallas kernels: 0 us -> 4.21 us
    gather x4 -> x0, local copies, waits for them, and re-layouts: 95.2 us -> none  [the longest x2 90.7 us: slot_ids(): ids = jnp.where(live, path_order[place], -1)]
    all_to_all x0 -> x4, blocking collectives: none -> 71.8 us  [spread(): return lax.all_to_all(rows, axes, 0, 0, tiled=True)]
    psum x4 -> x0, blocking collectives: 54.9 us -> none  [one_axis_at_a_time(): array = lax.psum(array, axis)]
    all_gather x1 -> x0, local copies, waits for them, and re-layouts: 10.7 us -> none  [body(): whole = lax.all_gather(frames, GY_GZ, axis=2, tiled=True)]
    reduce_sum x8 -> x0, other arithmetic: 4.64 us -> none  [the longest x1 1.98 us: cv_terms(): s_value = jnp.sum(progress_rank * weight)]
    pallas_call x0 -> x5, Pallas kernels: none -> 4.21 us  [call(): pl.pallas_call(kernel, out_shape=out_shape, out_specs=jax.tree.map(lambda...]
    another operation x3 -> x0, other arithmetic: 2.29 us -> none  [the longest x1 1.27 us: body(): return (forces, jnp.stack([s_value, z_value]))]
  transfers between devices with their start and end apart: 1 -> 0, of which waited for: 0 -> 0; matrix products, arithmetic and copies ran while one was open for 50% -> 0% of each run, Pallas kernels for 0% -> 0%
where the time goes in v2:
time: 77 us; the launch traced here: 76.7 us
  blocking collectives  71.8 us (93%)
  Pallas kernels  4.21 us (5%)
    all_to_all x4, blocking collectives, spread(): return lax.all_to_all(rows, axes, 0, 0, tiled=True)  71.8 us
    pallas_call x5, Pallas kernels, call(): pl.pallas_call(kernel, out_shape=out_shape, out_specs=jax.tree.map(lambda...  4.21 us

profile of v2, /device:TPU:1, one launch (start us, length us, event | category | flops | bytes accessed | tf_op | source)
XLA Modules:
  0.0 76.7 jit_solution(7763111665228879499)
XLA Ops:
  0.6 2.1 %pack.1 = (f32[128,128]{1,0:T(8,128)S(1)}, s32[3,128]{1,0:T(4,128)S(1)}, f32[3,128]{1,0:T(4,128)S(1)}, f32[3,512]{1,0:T(4,128)S(1)}) custom-call(s32[4,128]{1,0:T(4,128)} %bitcast.34, s32[32,128]{1,0:T(8,128)} %bitcast.33, s32[1,32]{1,0:T(1,128)} %slot_hbm.1, f32[3,512]{1,0:T(4,128)} %pos_hbm.1, s32[1,128]{1,0:T(1,128)} %bitcast.35), custom_call_target="tpu_custom_call" | custom-call | flops 2000000 | bytes 100000 | tf_op jit(solution)/shard_map/pack/pallas_call | solution.py:53
  2.8 0.0 copy-start
  2.8 29.8 %all_to_all.44 = f32[128,1,128]{2,1,0:T(1,128)S(1)} all-to-all(f32[128,1,128]{2,1,0:T(1,128)S(1)} %bitcast.27), channel_id=1, replica_groups=mesh['gx'=4,'gy'=8,'gz_0'=8,'gz_1'=2] {'gy','gz_0','gz_1'}, dimensions={0} | all-to-all | bytes 131072 | tf_op jit(solution)/shard_map/all_to_all | solution.py:220
  32.6 0.0 copy-done
  32.6 0.5 dist.1
  33.1 13.7 %all_to_all.45 = f32[32,1,128]{2,1,0:T(1,128)S(1)} all-to-all(f32[32,1,128]{2,1,0:T(1,128)S(1)} %bitcast.30), channel_id=1, replica_groups=mesh['gx'=4,'gy'=8,'gz_0'=8,'gz_1'=2] {'gx','gy'}, dimensions={0} | all-to-all | bytes 32768 | tf_op jit(solution)/shard_map/all_to_all | solution.py:220
  46.8 11.5 %all_to_all.46 = f32[16,1,128]{2,1,0:T(1,128)S(1)} all-to-all(f32[16,1,128]{2,1,0:T(1,128)S(1)} %bitcast.31), channel_id=1, replica_groups=mesh['gx'=4,'gy'=8,'gz_0'=8,'gz_1'=2] {'gz_0','gz_1'}, dimensions={0} | all-to-all | bytes 16384 | tf_op jit(solution)/shard_map/all_to_all | solution.py:220
  58.3 0.4 bias.1
  58.7 16.8 %all_to_all.47 = f32[128,1,128]{2,1,0:T(1,128)S(1)} all-to-all(f32[128,1,128]{2,1,0:T(1,128)S(1)} %bitcast.28), channel_id=1, replica_groups=mesh['gx'=4,'gy'=8,'gz_0'=8,'gz_1'=2] {'gy','gz_0','gz_1'}, dimensions={0} | all-to-all | bytes 131072 | tf_op jit(solution)/shard_map/all_to_all | solution.py:220
  75.5 1.2 %force.1 = (f32[3,512]{1,0:T(4,128)}, f32[1,2]{1,0:T(1,128)}) custom-call(f32[128,128]{1,0:T(8,128)S(1)} %bitcast.23, s32[3,128]{1,0:T(4,128)S(1)} %get-tuple-element.11.aux_ref, f32[3,128]{1,0:T(4,128)S(1)} %get-tuple-element.13.xyz_ref, f32[3,512]{1,0:T(4,128)S(1)} %get-tuple-element.14.pair_ref, f32[1,128]{1,0:T(1,128)S(1)} %get-tuple-element.15.cv_in_ref), custom_call_target="tpu_custom_call" | custom-call | flops 2000000 | bytes 100000 | tf_op jit(solution)/shard_map/force/pallas_call | solution.py:53
  (1 shorter events, 0.0 us)
Async XLA Ops:
  2.8 29.8 %copy-start = (f32[128,3,32]{0,2,1:T(8,128)S(1)}, f32[128,3,32]{0,2,1:T(8,128)}, u32[]{:S(2)}) copy-start(f32[128,3,32]{0,2,1:T(8,128)} %param.7) | copy-start | bytes 147460

commit v3 on v2

--- a/solution.py
+++ b/solution.py
@@ -2,6 +2,7 @@
 
 import jax
 import jax.numpy as jnp
+import numpy as np
 from jax import lax
 from jax.experimental import pallas as pl
 from jax.experimental.pallas import tpu as pltpu
@@ -17,11 +18,17 @@
 
 ALL = ("gx", "gy", "gz_0", "gz_1")
 HOLDERS = ("gy", "gz_0", "gz_1")
-N_HOLDERS = 128
-FIRST = ("gx", "gy")
-N_FIRST = 32
-SECOND = ("gz_0", "gz_1")
-N_SECOND = 16
+CHIPS = ("gy", "gz_0")
+N_CHIPS = 64
+IDS = 2 * BLOCK
+FIRST = ("gz_0", "gz_1")
+N_FIRST = 16
+SECOND = ("gx", "gy")
+N_SECOND = 32
+
+LEAD = {"gx": 2, "gy": 5, "gz_0": 4, "gz_1": 1}
+SIZE = {"gx": 4, "gy": 8, "gz_0": 8, "gz_1": 2}
+TURN = LEAD["gy"] * 8 + LEAD["gz_0"]
 
 STRENGTH = 20.0
 S_HOME = 0.5
@@ -106,7 +113,7 @@
     ]
     for copy in copies:
         copy.start()
-    here = lax.axis_index("gx") * N_HOLDERS + holder_index()
+    here = lax.axis_index("gx") * (2 * N_CHIPS) + holder_index()
     copies[0].wait()
     counts = count_ref[...]
     domain = iota(counts.shape, 0) * LANES + iota(counts.shape, 1)
@@ -143,7 +150,7 @@
     pair_forces(pos, pair_ref)
 
 
-def dist_kernel(got_ref, frames_ref, out_ref, coded):
+def dist_kernel(got_ref, mine_ref, other_ref, out_ref, coded):
     got = got_ref[...]
     part = iota(got.shape, 1) // SLOTS
     ids = jnp.where(part == 3, got, 0.0)
@@ -151,19 +158,22 @@
     ids = ids + pltpu.roll(ids, SLOTS, 1)
     coded[0] = ids
     coded[1] = jnp.where(part == 3, 1.0, got)
-    own = (holder_index() * BLOCK + iota((BLOCK, LANES), 0)).astype(F32)
-    found = [jnp.zeros((BLOCK, LANES), F32) for _ in range(2)]
-    for m in range(N_HOLDERS):
-        hit = jnp.where(coded[0, m : m + 1, :] == own, coded[1, m : m + 1, :], 0.0)
-        found[m % 2] = found[m % 2] + hit
-    found = found[0] + found[1]
-    part = iota((BLOCK, LANES), 1) // SLOTS
+    j = iota((IDS, LANES), 0)
+    own = ((holder_index() ^ (j // BLOCK)) * BLOCK + (j & (BLOCK - 1))).astype(F32)
+    found = jnp.zeros((IDS, LANES), F32)
+    for m in range(N_CHIPS):
+        found = found + jnp.where(coded[0, m : m + 1, :] == own, coded[1, m : m + 1, :], 0.0)
+    part = iota((IDS, LANES), 1) // SLOTS
     column = [jnp.sum(jnp.where(part == c, found, 0.0), axis=1, keepdims=True) for c in range(4)]
-    square = jnp.zeros((BLOCK, F), F32)
-    for c in range(3):
-        delta = column[c] - frames_ref[c * BLOCK : (c + 1) * BLOCK, :]
-        square = square + delta * delta
-    partial = jnp.sum(square * column[3], axis=0, keepdims=True) * (1.0 / P_SIZE)
+    total = jnp.zeros((BLOCK, F), F32)
+    for half, frames_ref in enumerate((mine_ref, other_ref)):
+        low = half * BLOCK
+        square = jnp.zeros((BLOCK, F), F32)
+        for c in range(3):
+            delta = column[c][low : low + BLOCK] - frames_ref[c * BLOCK : (c + 1) * BLOCK, :]
+            square = square + delta * delta
+        total = total + square * column[3][low : low + BLOCK]
+    partial = jnp.sum(total, axis=0, keepdims=True) * (1.0 / P_SIZE)
     out_ref[...] = jnp.broadcast_to(partial, out_ref.shape)
 
 
@@ -171,7 +181,7 @@
     out_ref[...] = jnp.broadcast_to(jnp.sum(got_ref[...], axis=0, keepdims=True), out_ref.shape)
 
 
-def bias_kernel(got_ref, aux_ref, frames_ref, out_ref, cv_ref):
+def bias_kernel(got_ref, aux_ref, mine_ref, other_ref, out_ref, cv_ref):
     dist = jnp.sum(got_ref[...], axis=0, keepdims=True)
     expo = -STRENGTH * dist
     top = jnp.max(expo, axis=1, keepdims=True)
@@ -189,17 +199,22 @@
     cv_ref[...] = jnp.where(lane == 0, s_value, z_value)
     eight = jnp.broadcast_to(grads, (8, F))
     dims = (((1,), (1,)), ((), ()))
-    own = lax.dot_general(eight, frames_ref[...], dims, precision=HIGHEST, preferred_element_type=F32)
     whole = jnp.broadcast_to(jnp.sum(grads, axis=1, keepdims=True), (1, BLOCK))
-    row = jnp.concatenate([own[0:1], whole], axis=1)
-    out_ref[...] = jnp.broadcast_to(row, out_ref.shape)
+    rows = []
+    for frames_ref in (mine_ref, other_ref):
+        sums = lax.dot_general(
+            eight, frames_ref[...], dims, precision=HIGHEST, preferred_element_type=F32
+        )
+        rows.append(jnp.concatenate([sums[0:1], whole], axis=1))
+    out_ref[...] = jnp.where((iota(out_ref.shape, 0) & 1) == 0, rows[0], rows[1])
 
 
 def force_kernel(got_ref, aux_ref, xyz_ref, pair_ref, cv_in_ref, out_ref, cv_ref):
     cv_ref[...] = cv_in_ref[:, 0:2]
     ids = aux_ref[0:1, 0:SLOTS]
     slots = aux_ref[1:2, 0:SLOTS]
-    from_row = (iota((N_HOLDERS, SLOTS), 0) == ids // BLOCK).astype(F32)
+    source = (ids // BLOCK) ^ (2 * TURN) ^ lax.axis_index("gz_1")
+    from_row = (iota((2 * N_CHIPS, SLOTS), 0) == source).astype(F32)
     dims = (((0,), (0,)), ((), ()))
     rows = lax.dot_general(got_ref[...], from_row, dims, precision=HIGHEST, preferred_element_type=F32)
     at = (iota((BLOCK, SLOTS), 0) == (ids & (BLOCK - 1))).astype(F32)
@@ -216,12 +231,22 @@
     out_ref[...] = pair_ref[...] + scattered[0:3]
 
 
+def groups_of(axes):
+    index = np.arange(math.prod(SIZE.values())).reshape(tuple(SIZE.values()))
+    rest = [n for n, axis in enumerate(ALL) if axis not in axes]
+    for axis in axes:
+        index = np.take(index, np.arange(SIZE[axis]) ^ LEAD[axis], axis=ALL.index(axis))
+    index = np.transpose(index, rest + [ALL.index(axis) for axis in axes])
+    return index.reshape(-1, math.prod(SIZE[axis] for axis in axes)).tolist()
+
+
 def spread(rows, axes):
-    return lax.all_to_all(rows, axes, 0, 0, tiled=True)
+    return lax.all_to_all(rows, ALL, 0, 0, tiled=True, axis_index_groups=groups_of(axes))
 
 
 def body(positions, frames, path_slot, path_count, path_order, frame_rank):
-    frames = jnp.transpose(frames, (1, 2, 0)).reshape(3 * BLOCK, F)
+    mine = jnp.transpose(frames, (1, 2, 0)).reshape(3 * BLOCK, F)
+    other = lax.ppermute(mine, "gz_1", [(0, 1), (1, 0)])
     inputs = (
         path_count.reshape(4, LANES),
         path_order.reshape(32, LANES),
@@ -233,7 +258,7 @@
     sent, aux, xyz, pair = call(
         pack_kernel,
         (
-            shaped(N_HOLDERS, LANES),
+            shaped(N_CHIPS, LANES),
             shaped(3, LANES, dtype=I32),
             shaped(3, LANES),
             shaped(3, ATOMS_LOCAL),
@@ -245,16 +270,19 @@
         + [pltpu.SemaphoreType.DMA((len(inputs),))],
         compiler_params=pltpu.CompilerParams(vmem_limit_bytes=8 << 20),
     )
-    atoms = spread(sent, HOLDERS)
-    coded = [pltpu.VMEM((2, N_HOLDERS, LANES), F32)]
-    partial = small(dist_kernel, shaped(N_FIRST, LANES), "dist", (atoms, frames), coded)
+    atoms = spread(sent, CHIPS)
+    coded = [pltpu.VMEM((2, N_CHIPS, LANES), F32)]
+    partial = small(dist_kernel, shaped(N_FIRST, LANES), "dist", (atoms, mine, other), coded)
     first = spread(partial, FIRST)
     row_sum = small(sum_kernel, shaped(N_SECOND, LANES), "sum", (first,))
     second = spread(row_sum, SECOND)
     biases, cv = small(
-        bias_kernel, (shaped(N_HOLDERS, LANES), shaped(1, LANES)), "bias", (second, aux, frames)
-    )
-    back = spread(biases, HOLDERS)
+        bias_kernel,
+        (shaped(2 * N_CHIPS, LANES), shaped(1, LANES)),
+        "bias",
+        (second, aux, mine, other),
+    )
+    back = spread(biases, CHIPS)
     forces, cv = small(
         force_kernel, (shaped(3, ATOMS_LOCAL), shaped(1, 2)), "force", (back, aux, xyz, pair, cv)
     )

time: 77 us -> 66.2 us (0.86)
  the two profiles are of different devices: /device:TPU:1 before, /device:TPU:2 now
where the time goes in v3:
time: 66.2 us; the launch traced here: 65.9 us
  blocking collectives  38.6 us (58%)
  starting transfers between devices  20.9 us (32%)
  Pallas kernels  4.33 us (7%)
  waiting for transfers between devices  1.31 us (2%)
  between operations  0.68 us (1%)
    all_to_all x3, blocking collectives, spread(): lax.all_to_all(rows, ALL, 0, 0, tiled=True, axis_index_groups=groups_of(a...  38.6 us
    all_to_all x1, starting transfers between devices, spread(): lax.all_to_all(rows, ALL, 0, 0, tiled=True, axis_index_groups=groups_of(a...  19 us
    pallas_call x5, Pallas kernels, call(): pl.pallas_call(kernel, out_shape=out_shape, out_specs=jax.tree.map(lambda...  4.33 us
    ppermute x1, starting transfers between devices, body(): other = lax.ppermute(mine, 'gz_1', [(0, 1), (1, 0)])  1.92 us
  transfers between devices with their start and end apart: 2, of which 2 were waited for; matrix products, arithmetic and copies ran while one was open for 0% of the time, Pallas kernels for 0%

profile of v3, /device:TPU:2, one launch (start us, length us, event | category | flops | bytes accessed | tf_op | source)
XLA Modules:
  0.0 65.9 jit_solution(8488792075239678647)
XLA Ops:
  0.6 0.0 copy-start
  0.6 2.1 %pack.1 = (f32[64,128]{1,0:T(8,128)}, s32[3,128]{1,0:T(4,128)S(1)}, f32[3,128]{1,0:T(4,128)S(1)}, f32[3,512]{1,0:T(4,128)S(1)}) custom-call(s32[4,128]{1,0:T(4,128)} %bitcast.32, s32[32,128]{1,0:T(8,128)} %bitcast.31, s32[1,32]{1,0:T(1,128)} %slot_hbm.1, f32[3,512]{1,0:T(4,128)} %pos_hbm.1, s32[1,128]{1,0:T(1,128)} %bitcast.33), custom_call_target="tpu_custom_call" | custom-call | flops 2000000 | bytes 100000 | tf_op jit(solution)/shard_map/pack/pallas_call | solution.py:60
  2.8 19.0 %all-to-all-start = ((f32[64,1,128]{2,1,0:T(1,128)}), f32[64,1,128]{2,1,0:T(1,128)S(1)}, u32[]{:S(2)}, u32[]{:S(2)}) async-start(f32[64,1,128]{2,1,0:T(1,128)} %bitcast.4), calls=%async_computation | async-start | bytes 65536 | tf_op jit(solution)/shard_map/all_to_all | solution.py:244
  21.8 0.0 copy-done
  21.8 1.9 %collective-permute-start = (f32[96,128]{1,0:T(8,128)S(1)}, f32[96,128]{1,0:T(8,128)S(1)}, u32[]{:S(2)}, u32[]{:S(2)}) collective-permute-start(f32[96,128]{1,0:T(8,128)S(1)} %bitcast.22), channel_id=1, source_target_pairs={{0,1},{1,0},{2,3},{3,2},{4,5},{5,4},{6,7},{7,6},{8,9},{9,8},{10,11... | collective-permute-start | bytes 147464 | tf_op jit(solution)/shard_map/ppermute | solution.py:249
  23.8 1.2 %collective-permute-done.other_ref = f32[96,128]{1,0:T(8,128)S(1)} collective-permute-done((f32[96,128]{1,0:T(8,128)S(1)}, f32[96,128]{1,0:T(8,128)S(1)}, u32[]{:S(2)}, u32[]{:S(2)}) %collective-permute-start) | collective-permute-done | bytes 49184 | tf_op jit(solution)/shard_map/ppermute | solution.py:249
  25.0 0.1 all-to-all-done
  25.1 0.5 dist.1
  25.5 9.6 %all_to_all.44 = f32[16,1,128]{2,1,0:T(1,128)S(1)} all-to-all(f32[16,1,128]{2,1,0:T(1,128)S(1)} %bitcast.29), channel_id=1, replica_groups={{9,8,11,10,13,12,15,14,1,0,3,2,5,4,7,6},{25,24,27,26,29,28,31,30,17,16,..., dimensions={0} | all-to-all | bytes 16384 | tf_op jit(solution)/shard_map/all_to_all | solution.py:244
  35.1 12.8 %all_to_all.45 = f32[32,1,128]{2,1,0:T(1,128)S(1)} all-to-all(f32[32,1,128]{2,1,0:T(1,128)S(1)} %bitcast.28), channel_id=1, replica_groups={{336,320,368,352,272,256,304,288,464,448,496,480,400,384,432,416,80,64,..., dimensions={0} | all-to-all | bytes 32768 | tf_op jit(solution)/shard_map/all_to_all | solution.py:244
  48.0 0.5 bias.1
  48.5 16.2 %all_to_all.46 = f32[64,2,128]{2,1,0:T(2,128)S(1)} all-to-all(f32[64,2,128]{2,1,0:T(2,128)S(1)} %bitcast.27), channel_id=1, replica_groups={{88,90,92,94,80,82,84,86,72,74,76,78,64,66,68,70,120,122,124,126,112,11..., dimensions={0} | all-to-all | bytes 131072 | tf_op jit(solution)/shard_map/all_to_all | solution.py:244
  64.7 1.2 %force.1 = (f32[3,512]{1,0:T(4,128)}, f32[1,2]{1,0:T(1,128)}) custom-call(f32[128,128]{1,0:T(8,128)S(1)} %bitcast.21, s32[3,128]{1,0:T(4,128)S(1)} %get-tuple-element.11.aux_ref, f32[3,128]{1,0:T(4,128)S(1)} %get-tuple-element.13.xyz_ref, f32[3,512]{1,0:T(4,128)S(1)} %get-tuple-element.14.pair_ref, f32[1,128]{1,0:T(1,128)S(1)} %get-tuple-element.15.cv_in_ref), custom_call_target="tpu_custom_call" | custom-call | flops 2000000 | bytes 100000 | tf_op jit(solution)/shard_map/force/pallas_call | solution.py:60
  (1 shorter events, 0.0 us)
Async XLA Ops:
  0.6 21.2 %copy-start = (f32[128,3,32]{0,2,1:T(8,128)S(1)}, f32[128,3,32]{0,2,1:T(8,128)}, u32[]{:S(2)}) copy-start(f32[128,3,32]{0,2,1:T(8,128)} %param.7) | copy-start | bytes 147460
  2.8 22.3 %all-to-all-start = ((f32[64,1,128]{2,1,0:T(1,128)}), f32[64,1,128]{2,1,0:T(1,128)S(1)}, u32[]{:S(2)}, u32[]{:S(2)}) async-start(f32[64,1,128]{2,1,0:T(1,128)} %bitcast.4), calls=%async_computation | async-start | bytes 65536 | tf_op jit(solution)/shard_map/all_to_all | solution.py:244
  21.8 3.1 %collective-permute-start = (f32[96,128]{1,0:T(8,128)S(1)}, f32[96,128]{1,0:T(8,128)S(1)}, u32[]{:S(2)}, u32[]{:S(2)}) collective-permute-start(f32[96,128]{1,0:T(8,128)S(1)} %bitcast.22), channel_id=1, source_target_pairs={{0,1},{1,0},{2,3},{3,2},{4,5},{5,4},{6,7},{7,6},{8,9},{9,8},{10,11... | collective-permute-start | bytes 147464 | tf_op jit(solution)/shard_map/ppermute | solution.py:249

commit v4 on v3

--- a/solution.py
+++ b/solution.py
@@ -2,12 +2,12 @@
 
 import jax
 import jax.numpy as jnp
-import numpy as np
 from jax import lax
 from jax.experimental import pallas as pl
 from jax.experimental.pallas import tpu as pltpu
 from jax.sharding import Mesh
 from jax.sharding import PartitionSpec as P
+
 
 P_SIZE = 4096
 F = 128
@@ -18,17 +18,19 @@
 
 ALL = ("gx", "gy", "gz_0", "gz_1")
 HOLDERS = ("gy", "gz_0", "gz_1")
-CHIPS = ("gy", "gz_0")
 N_CHIPS = 64
 IDS = 2 * BLOCK
-FIRST = ("gz_0", "gz_1")
 N_FIRST = 16
-SECOND = ("gx", "gy")
 N_SECOND = 32
 
-LEAD = {"gx": 2, "gy": 5, "gz_0": 4, "gz_1": 1}
-SIZE = {"gx": 4, "gy": 8, "gz_0": 8, "gz_1": 2}
-TURN = LEAD["gy"] * 8 + LEAD["gz_0"]
+X_FIRST, Y_FIRST = 2, 4
+Z_FIRST = (5, 5)
+TURN = tuple(16 * z + 2 * Y_FIRST for z in Z_FIRST)
+
+
+def middle(z):
+    return ((z + 2) & 4) // 4
+
 
 STRENGTH = 20.0
 S_HOME = 0.5
@@ -56,22 +58,20 @@
     return jax.ShapeDtypeStruct(shape, dtype)
 
 
-def call(kernel, out_shape, name, inputs, **kwargs):
+def call(kernel, out_shape, inputs, **kwargs):
     return pl.pallas_call(
         kernel,
         out_shape=out_shape,
         out_specs=jax.tree.map(lambda _: VMEM, out_shape),
-        name=name,
         cost_estimate=pl.CostEstimate(flops=2000000, bytes_accessed=100000, transcendentals=0),
         **kwargs,
     )(*inputs)
 
 
-def small(kernel, out_shape, name, inputs, scratch=()):
+def small(kernel, out_shape, inputs, scratch=()):
     return call(
         kernel,
         out_shape,
-        name,
         inputs,
         in_specs=[VMEM] * len(inputs),
         scratch_shapes=scratch,
@@ -79,7 +79,8 @@
     )
 
 
-def pair_forces(pos, out_ref):
+def pair_kernel(pos_ref, out_ref):
+    pos = pos_ref[...]
     columns = jnp.transpose(jnp.concatenate([pos, pos[0:1]] * 2, axis=0))
     scale = -1.0 / (WIDTH_SQ * math.log(2.0))
     step = 64
@@ -97,7 +98,7 @@
 
 
 def pack_kernel(
-    count_hbm, order_hbm, slot_hbm, pos_hbm, rank_hbm, out_ref, aux_ref, xyz_ref, pair_ref, count_ref, order_ref, slot_ref, pos_ref, rank_ref, sems
+    count_hbm, order_hbm, slot_hbm, pos_hbm, rank_hbm, out_ref, aux_ref, xyz_ref, pos_out_ref, count_ref, order_ref, slot_ref, pos_ref, rank_ref, sems
 ):
     copies = [
         pltpu.make_async_copy(source, target, sems.at[i])
@@ -114,40 +115,39 @@
     for copy in copies:
         copy.start()
     here = lax.axis_index("gx") * (2 * N_CHIPS) + holder_index()
-    copies[0].wait()
+    for copy in copies:
+        copy.wait()
     counts = count_ref[...]
     domain = iota(counts.shape, 0) * LANES + iota(counts.shape, 1)
     offset = jnp.sum(jnp.where(domain < here, counts, 0))
-    mine = jnp.sum(jnp.where(domain == here, counts, 0))
-    copies[1].wait()
+    mine = jnp.where(domain == here, counts, 0)
+    mine = jnp.sum(jnp.sum(mine, axis=0, keepdims=True), axis=1, keepdims=True)
+    slots = jnp.concatenate([slot_ref[...]] * 4, axis=1)
+    pick = (iota((ATOMS_LOCAL, LANES), 0) == slots).astype(F32)
+    pos = pos_ref[...]
+    xyz = jnp.dot(pos, pick, precision=HIGHEST, preferred_element_type=F32)
+    lane = iota((1, LANES), 1)
+    k = lane & (SLOTS - 1)
+    live = k < mine
     row = offset // LANES
     shift = offset - row * LANES
     first = order_ref[pl.ds(row, 1), :]
     second = order_ref[pl.ds(jnp.minimum(row + 1, P_SIZE // LANES - 1), 1), :]
-    lane = iota((1, LANES), 1)
-    k = lane & (SLOTS - 1)
-    turn = jnp.where(shift == 0, 0, LANES - shift)
-    ids = jnp.where(lane < LANES - shift, pltpu.roll(first, turn, 1), pltpu.roll(second, turn, 1))
-    ids = jnp.where(lane < SLOTS, ids, 0)
-    copies[2].wait()
-    slots = jnp.concatenate([slot_ref[...]] * 4, axis=1)
-    ids = ids + pltpu.roll(ids, 2 * SLOTS, 1)
-    ids = ids + pltpu.roll(ids, SLOTS, 1)
-    live = k < mine
-    ids = jnp.where(live, ids, -1)
-    pick = (iota((ATOMS_LOCAL, LANES), 0) == slots).astype(F32)
-    copies[3].wait()
-    pos = pos_ref[...]
-    xyz = jnp.dot(pos, pick, precision=HIGHEST, preferred_element_type=F32)
+    ids = jnp.full((1, LANES), -1, I32)
+    for part in range(4):
+        start = shift - part * SLOTS
+        turn = jnp.where(start <= 0, -start, LANES - start)
+        here_first = k < LANES - shift
+        turned = jnp.where(here_first, pltpu.roll(first, turn, 1), pltpu.roll(second, turn, 1))
+        ids = jnp.where(live & (lane // SLOTS == part), turned, ids)
     xyz_ref[...] = xyz
     part = lane // SLOTS
     row_out = jnp.where(part == 0, xyz[0:1], jnp.where(part == 1, xyz[1:2], xyz[2:3]))
     row_out = jnp.where(live, row_out, 0.0)
     row_out = jnp.where(part == 3, ids.astype(F32), row_out)
     out_ref[...] = jnp.broadcast_to(row_out, out_ref.shape)
-    copies[4].wait()
     aux_ref[...] = jnp.concatenate([ids, slots, rank_ref[...]], axis=0)
-    pair_forces(pos, pair_ref)
+    pos_out_ref[...] = pos
 
 
 def dist_kernel(got_ref, mine_ref, other_ref, out_ref, coded):
@@ -186,11 +186,12 @@
     expo = -STRENGTH * dist
     top = jnp.max(expo, axis=1, keepdims=True)
     expd = jnp.exp(expo - top)
+    rank = aux_ref[2:3, :].astype(F32) / (F - 1.0)
     total = jnp.sum(expd, axis=1, keepdims=True)
+    ranked = jnp.sum(rank * expd, axis=1, keepdims=True)
+    s_value = ranked / total
+    z_value = -(top + jnp.log(total)) / STRENGTH
     weight = expd / total
-    rank = aux_ref[2:3, :].astype(F32) / (F - 1.0)
-    s_value = jnp.sum(rank * weight, axis=1, keepdims=True)
-    z_value = -(top + jnp.log(total)) / STRENGTH
     grads = (
         KAPPA_S * P_SIZE * (s_value - S_HOME) * -STRENGTH * weight * (rank - s_value)
         + KAPPA_Z * P_SIZE * z_value * weight
@@ -199,13 +200,12 @@
     cv_ref[...] = jnp.where(lane == 0, s_value, z_value)
     eight = jnp.broadcast_to(grads, (8, F))
     dims = (((1,), (1,)), ((), ()))
-    whole = jnp.broadcast_to(jnp.sum(grads, axis=1, keepdims=True), (1, BLOCK))
+    ones = jnp.ones((BLOCK, F), F32)
     rows = []
     for frames_ref in (mine_ref, other_ref):
-        sums = lax.dot_general(
-            eight, frames_ref[...], dims, precision=HIGHEST, preferred_element_type=F32
-        )
-        rows.append(jnp.concatenate([sums[0:1], whole], axis=1))
+        against = jnp.concatenate([frames_ref[...], ones], axis=0)
+        sums = lax.dot_general(eight, against, dims, precision=HIGHEST, preferred_element_type=F32)
+        rows.append(sums[0:1])
     out_ref[...] = jnp.where((iota(out_ref.shape, 0) & 1) == 0, rows[0], rows[1])
 
 
@@ -213,7 +213,9 @@
     cv_ref[...] = cv_in_ref[:, 0:2]
     ids = aux_ref[0:1, 0:SLOTS]
     slots = aux_ref[1:2, 0:SLOTS]
-    source = (ids // BLOCK) ^ (2 * TURN) ^ lax.axis_index("gz_1")
+    half = lax.axis_index("gz_1") ^ middle(lax.axis_index("gy"))
+    turn = TURN[0] + half * (TURN[1] - TURN[0])
+    source = (ids // BLOCK) ^ turn ^ half ^ middle(ids // (16 * BLOCK))
     from_row = (iota((2 * N_CHIPS, SLOTS), 0) == source).astype(F32)
     dims = (((0,), (0,)), ((), ()))
     rows = lax.dot_general(got_ref[...], from_row, dims, precision=HIGHEST, preferred_element_type=F32)
@@ -231,17 +233,44 @@
     out_ref[...] = pair_ref[...] + scattered[0:3]
 
 
-def groups_of(axes):
-    index = np.arange(math.prod(SIZE.values())).reshape(tuple(SIZE.values()))
-    rest = [n for n, axis in enumerate(ALL) if axis not in axes]
-    for axis in axes:
-        index = np.take(index, np.arange(SIZE[axis]) ^ LEAD[axis], axis=ALL.index(axis))
-    index = np.transpose(index, rest + [ALL.index(axis) for axis in axes])
-    return index.reshape(-1, math.prod(SIZE[axis] for axis in axes)).tolist()
-
-
-def spread(rows, axes):
-    return lax.all_to_all(rows, ALL, 0, 0, tiled=True, axis_index_groups=groups_of(axes))
+def device(x, z, y, core):
+    return ((x * 8 + z) * 8 + y) * 2 + core
+
+
+def chip_groups():
+    return [
+        [
+            device(x, z ^ Z_FIRST[half], y ^ Y_FIRST, half ^ middle(z ^ Z_FIRST[half]))
+            for z in range(8)
+            for y in range(8)
+        ]
+        for x in range(4)
+        for half in range(2)
+    ]
+
+
+def first_groups():
+    return [
+        [device(x, z, y ^ Y_FIRST, core ^ 1) for y in range(8) for core in range(2)]
+        for x in range(4)
+        for z in range(8)
+    ]
+
+
+def second_groups():
+    return [
+        [
+            device(x ^ X_FIRST, z ^ Z_FIRST[half], y, half ^ middle(z ^ Z_FIRST[half]))
+            for x in range(4)
+            for z in range(8)
+        ]
+        for y in range(8)
+        for half in range(2)
+    ]
+
+
+def spread(rows, groups):
+    return lax.all_to_all(rows, ALL, 0, 0, tiled=True, axis_index_groups=groups)
 
 
 def body(positions, frames, path_slot, path_count, path_order, frame_rank):
@@ -255,7 +284,7 @@
         frame_rank.reshape(1, F),
     )
     inputs = tuple(pltpu.with_memory_space_constraint(a, pltpu.HBM) for a in inputs)
-    sent, aux, xyz, pair = call(
+    sent, aux, xyz, pos = call(
         pack_kernel,
         (
             shaped(N_CHIPS, LANES),
@@ -263,28 +292,25 @@
             shaped(3, LANES),
             shaped(3, ATOMS_LOCAL),
         ),
-        "pack",
         inputs,
         in_specs=[HBM] * len(inputs),
         scratch_shapes=[pltpu.VMEM(a.shape, a.dtype) for a in inputs]
         + [pltpu.SemaphoreType.DMA((len(inputs),))],
         compiler_params=pltpu.CompilerParams(vmem_limit_bytes=8 << 20),
     )
-    atoms = spread(sent, CHIPS)
+    atoms = spread(sent, chip_groups())
     coded = [pltpu.VMEM((2, N_CHIPS, LANES), F32)]
-    partial = small(dist_kernel, shaped(N_FIRST, LANES), "dist", (atoms, mine, other), coded)
-    first = spread(partial, FIRST)
-    row_sum = small(sum_kernel, shaped(N_SECOND, LANES), "sum", (first,))
-    second = spread(row_sum, SECOND)
+    partial = small(dist_kernel, shaped(N_FIRST, LANES), (atoms, mine, other), coded)
+    first = spread(partial, first_groups())
+    row_sum = small(sum_kernel, shaped(N_SECOND, LANES), (first,))
+    second = spread(row_sum, second_groups())
     biases, cv = small(
-        bias_kernel,
-        (shaped(2 * N_CHIPS, LANES), shaped(1, LANES)),
-        "bias",
-        (second, aux, mine, other),
-    )
-    back = spread(biases, CHIPS)
+        bias_kernel, (shaped(2 * N_CHIPS, LANES), shaped(1, LANES)), (second, aux, mine, other)
+    )
+    back = spread(biases, chip_groups())
+    pair = small(pair_kernel, shaped(3, ATOMS_LOCAL), (pos,))
     forces, cv = small(
-        force_kernel, (shaped(3, ATOMS_LOCAL), shaped(1, 2)), "force", (back, aux, xyz, pair, cv)
+        force_kernel, (shaped(3, ATOMS_LOCAL), shaped(1, 2)), (back, aux, xyz, pair, cv)
     )
     return forces, cv.reshape(2)
 

time: 66.2 us -> 67.2 us (1.015)
  the two profiles are of different devices: /device:TPU:2 before, /device:TPU:1 now
where the time goes in v4:
time: 67.2 us; the launch traced here: 66.9 us
  starting transfers between devices  35.4 us (53%)
  blocking collectives  22 us (33%)
  Pallas kernels  5.31 us (8%)
  waiting for transfers between devices  3.4 us (5%)
  between operations  0.69 us (1%)
    all_to_all x2, starting transfers between devices, spread(): return lax.all_to_all(rows, ALL, 0, 0, tiled=True, axis_index_groups=groups)  33 us
    all_to_all x2, blocking collectives, spread(): return lax.all_to_all(rows, ALL, 0, 0, tiled=True, axis_index_groups=groups)  22 us
    pallas_call x6, Pallas kernels, call(): pl.pallas_call(kernel, out_shape=out_shape, out_specs=jax.tree.map(lambda...  5.31 us
    all_to_all x2, waiting for transfers between devices, spread(): return lax.all_to_all(rows, ALL, 0, 0, tiled=True, axis_index_groups=groups)  2.54 us
    ppermute x1, starting transfers between devices, body(): other = lax.ppermute(mine, 'gz_1', [(0, 1), (1, 0)])  2.43 us
  transfers between devices with their start and end apart: 3, of which 2 were waited for; matrix products, arithmetic and copies ran while one was open for 0% of the time, Pallas kernels for 1%

profile of v4, /device:TPU:1, one launch (start us, length us, event | category | flops | bytes accessed | tf_op | source)
XLA Modules:
  0.0 66.9 jit_solution(11763791102013410300)
XLA Ops:
  0.6 0.0 copy-start
  0.6 1.7 %shard_map.77 = (f32[64,128]{1,0:T(8,128)}, s32[3,128]{1,0:T(4,128)S(1)}, f32[3,128]{1,0:T(4,128)S(1)}, f32[3,512]{1,0:T(4,128)S(1)}) custom-call(s32[4,128]{1,0:T(4,128)} %bitcast.31, s32[32,128]{1,0:T(8,128)} %bitcast.30, s32[1,32]{1,0:T(1,128)} %slot_hbm.1, f32[3,512]{1,0:T(4,128)} %pos_hbm.1, s32[1,128]{1,0:T(1,128)} %bitcast.32), custom_call_target="tpu_custom_call" | custom-call | flops 2000000 | bytes 100000 | tf_op jit(solution)/shard_map/pallas_call | solution.py:62
  2.4 19.7 %all-to-all-start = ((f32[64,1,128]{2,1,0:T(1,128)}), f32[64,1,128]{2,1,0:T(1,128)S(1)}, u32[]{:S(2)}, u32[]{:S(2)}) async-start(f32[64,1,128]{2,1,0:T(1,128)} %bitcast.4), calls=%async_computation | async-start | bytes 65536 | tf_op jit(solution)/shard_map/all_to_all | solution.py:273
  22.1 0.0 copy-done
  22.1 2.4 %collective-permute-start = (f32[96,128]{1,0:T(8,128)S(1)}, f32[96,128]{1,0:T(8,128)S(1)}, u32[]{:S(2)}, u32[]{:S(2)}) collective-permute-start(f32[96,128]{1,0:T(8,128)S(1)} %bitcast.22), channel_id=1, source_target_pairs={{0,1},{1,0},{2,3},{3,2},{4,5},{5,4},{6,7},{7,6},{8,9},{9,8},{10,11... | collective-permute-start | bytes 147464 | tf_op jit(solution)/shard_map/ppermute | solution.py:278
  24.6 0.9 %collective-permute-done.other_ref = f32[96,128]{1,0:T(8,128)S(1)} collective-permute-done((f32[96,128]{1,0:T(8,128)S(1)}, f32[96,128]{1,0:T(8,128)S(1)}, u32[]{:S(2)}, u32[]{:S(2)}) %collective-permute-start) | collective-permute-done | bytes 49184 | tf_op jit(solution)/shard_map/ppermute | solution.py:278
  25.4 0.0 all-to-all-done
  25.4 0.5 shard_map.78
  25.9 9.3 %all_to_all.44 = f32[16,1,128]{2,1,0:T(1,128)S(1)} all-to-all(f32[16,1,128]{2,1,0:T(1,128)S(1)} %bitcast.28), channel_id=1, replica_groups={{9,8,11,10,13,12,15,14,1,0,3,2,5,4,7,6},{25,24,27,26,29,28,31,30,17,16,..., dimensions={0} | all-to-all | bytes 16384 | tf_op jit(solution)/shard_map/all_to_all | solution.py:273
  35.2 12.7 %all_to_all.45 = f32[32,1,128]{2,1,0:T(1,128)S(1)} all-to-all(f32[32,1,128]{2,1,0:T(1,128)S(1)} %bitcast.27), channel_id=1, replica_groups={{337,321,368,352,272,256,305,289,465,449,496,480,400,384,433,417,81,65,..., dimensions={0} | all-to-all | bytes 32768 | tf_op jit(solution)/shard_map/all_to_all | solution.py:273
  47.9 1.1 %shard_map.80 = (f32[128,128]{1,0:T(8,128)}, f32[1,128]{1,0:T(1,128)S(1)}) custom-call(f32[32,128]{1,0:T(8,128)S(1)} %bitcast.26, s32[3,128]{1,0:T(4,128)S(1)} %get-tuple-element.11.aux_ref, f32[96,128]{1,0:T(8,128)S(1)} %bitcast.24, f32[96,128]{1,0:T(8,128)S(1)} %collective-permute-done.other_ref), custom_call_target="tpu_custom_call" | custom-call | flops 2000000 | bytes 100000 | tf_op jit(solution)/shard_map/pallas_call | solution.py:62
  49.0 13.3 %all-to-all-start.3 = ((f32[64,2,128]{2,1,0:T(2,128)}), f32[64,2,128]{2,1,0:T(2,128)S(1)}, u32[]{:S(2)}, u32[]{:S(2)}) async-start(f32[64,2,128]{2,1,0:T(2,128)} %bitcast.15), calls=%async_computation.3 | async-start | bytes 131072 | tf_op jit(solution)/shard_map/all_to_all | solution.py:273
  62.3 0.8 %shard_map.81.pair_ref = f32[3,512]{1,0:T(4,128)S(1)} custom-call(f32[3,512]{1,0:T(4,128)S(1)} %get-tuple-element.14.pos_ref), custom_call_target="tpu_custom_call" | custom-call | flops 2000000 | bytes 100000 | tf_op jit(solution)/shard_map/pallas_call | solution.py:62
  63.1 2.5 %all-to-all-done.3 = f32[64,2,128]{2,1,0:T(2,128)S(1)} async-done(((f32[64,2,128]{2,1,0:T(2,128)}), f32[64,2,128]{2,1,0:T(2,128)S(1)}, u32[]{:S(2)}, u32[]{:S(2)}) %all-to-all-start.3) | async-done | bytes 65568 | tf_op jit(solution)/shard_map/all_to_all | solution.py:273
  65.6 1.2 %shard_map.82 = (f32[3,512]{1,0:T(4,128)}, f32[1,2]{1,0:T(1,128)}) custom-call(f32[128,128]{1,0:T(8,128)S(1)} %bitcast.21, s32[3,128]{1,0:T(4,128)S(1)} %get-tuple-element.11.aux_ref, f32[3,128]{1,0:T(4,128)S(1)} %get-tuple-element.13.xyz_ref, f32[3,512]{1,0:T(4,128)S(1)} %shard_map.81.pair_ref, f32[1,128]{1,0:T(1,128)S(1)} %get-tuple-element.15.cv_in_ref), custom_call_target="tpu_custom_call" | custom-call | flops 2000000 | bytes 100000 | tf_op jit(solution)/shard_map/pallas_call | solution.py:62
  (1 shorter events, 0.0 us)
Async XLA Ops:
  0.6 21.5 %copy-start = (f32[128,3,32]{0,2,1:T(8,128)S(1)}, f32[128,3,32]{0,2,1:T(8,128)}, u32[]{:S(2)}) copy-start(f32[128,3,32]{0,2,1:T(8,128)} %param.7) | copy-start | bytes 147460
  2.4 23.0 %all-to-all-start = ((f32[64,1,128]{2,1,0:T(1,128)}), f32[64,1,128]{2,1,0:T(1,128)S(1)}, u32[]{:S(2)}, u32[]{:S(2)}) async-start(f32[64,1,128]{2,1,0:T(1,128)} %bitcast.4), calls=%async_computation | async-start | bytes 65536 | tf_op jit(solution)/shard_map/all_to_all | solution.py:273
  22.1 3.3 %collective-permute-start = (f32[96,128]{1,0:T(8,128)S(1)}, f32[96,128]{1,0:T(8,128)S(1)}, u32[]{:S(2)}, u32[]{:S(2)}) collective-permute-start(f32[96,128]{1,0:T(8,128)S(1)} %bitcast.22), channel_id=1, source_target_pairs={{0,1},{1,0},{2,3},{3,2},{4,5},{5,4},{6,7},{7,6},{8,9},{9,8},{10,11... | collective-permute-start | bytes 147464 | tf_op jit(solution)/shard_map/ppermute | solution.py:278
  49.0 16.6 %all-to-all-start.3 = ((f32[64,2,128]{2,1,0:T(2,128)}), f32[64,2,128]{2,1,0:T(2,128)S(1)}, u32[]{:S(2)}, u32[]{:S(2)}) async-start(f32[64,2,128]{2,1,0:T(2,128)} %bitcast.15), calls=%async_computation.3 | async-start | bytes 131072 | tf_op jit(solution)/shard_map/all_to_all | solution.py:273

commit v5 on v4

--- a/solution.py
+++ b/solution.py
@@ -23,9 +23,11 @@
 N_FIRST = 16
 N_SECOND = 32
 
-X_FIRST, Y_FIRST = 2, 4
-Z_FIRST = (5, 5)
-TURN = tuple(16 * z + 2 * Y_FIRST for z in Z_FIRST)
+ATOMS_FIRST = (5, 5)
+FIRST_FIRST = 4
+SECOND_FIRST = (2, 5)
+BIAS_FIRST = (4, 4)
+TURN = 16 * BIAS_FIRST[0] + 2 * BIAS_FIRST[1]
 
 
 def middle(z):
@@ -79,7 +81,21 @@
     )
 
 
-def pair_kernel(pos_ref, out_ref):
+def pair_kernel(pos_ref, aux_ref, xyz_ref, out_ref, select_ref, part_ref, pick_ref):
+    columns = [aux_ref[0:2, :].astype(F32), xyz_ref[...], xyz_ref[...]]
+    columns = jnp.transpose(jnp.concatenate(columns, axis=0))[0:SLOTS]
+    ids = columns[:, 0:1].astype(I32)
+    slots = columns[:, 1:2].astype(I32)
+    half = lax.axis_index("gz_1") ^ middle(lax.axis_index("gy"))
+    source = (ids // BLOCK) ^ TURN ^ half ^ middle(ids // (16 * BLOCK))
+    lane = iota((SLOTS, LANES), 1)
+    select_ref[...] = (lane == source).astype(F32)
+    scale = jnp.where(ids >= 0, -2.0 / P_SIZE, 0.0)
+    for c in range(3):
+        at = (lane == c * BLOCK + (ids & (BLOCK - 1))).astype(F32)
+        whole = jnp.where(lane == 3 * BLOCK, columns[:, c + 2 : c + 3], 0.0)
+        part_ref[c * SLOTS : (c + 1) * SLOTS, :] = scale * (whole - at)
+    pick_ref[...] = (iota((SLOTS, ATOMS_LOCAL), 1) == slots).astype(F32)
     pos = pos_ref[...]
     columns = jnp.transpose(jnp.concatenate([pos, pos[0:1]] * 2, axis=0))
     scale = -1.0 / (WIDTH_SQ * math.log(2.0))
@@ -209,38 +225,32 @@
     out_ref[...] = jnp.where((iota(out_ref.shape, 0) & 1) == 0, rows[0], rows[1])
 
 
-def force_kernel(got_ref, aux_ref, xyz_ref, pair_ref, cv_in_ref, out_ref, cv_ref):
+def force_kernel(got_ref, select_ref, part_ref, pick_ref, pair_ref, cv_in_ref, out_ref, cv_ref):
     cv_ref[...] = cv_in_ref[:, 0:2]
-    ids = aux_ref[0:1, 0:SLOTS]
-    slots = aux_ref[1:2, 0:SLOTS]
-    half = lax.axis_index("gz_1") ^ middle(lax.axis_index("gy"))
-    turn = TURN[0] + half * (TURN[1] - TURN[0])
-    source = (ids // BLOCK) ^ turn ^ half ^ middle(ids // (16 * BLOCK))
-    from_row = (iota((2 * N_CHIPS, SLOTS), 0) == source).astype(F32)
-    dims = (((0,), (0,)), ((), ()))
-    rows = lax.dot_general(got_ref[...], from_row, dims, precision=HIGHEST, preferred_element_type=F32)
-    at = (iota((BLOCK, SLOTS), 0) == (ids & (BLOCK - 1))).astype(F32)
-    whole = rows[96:97]
-    bias = []
+    got = got_ref[...]
+    high = got.astype(jnp.bfloat16)
+    rest = got - high.astype(F32)
+    mid = rest.astype(jnp.bfloat16)
+    low = (rest - mid.astype(F32)).astype(jnp.bfloat16)
+    select = select_ref[...].astype(jnp.bfloat16)
+    rows = [jnp.dot(select, piece, preferred_element_type=F32) for piece in (low, mid, high)]
+    rows = (rows[0] + rows[1]) + rows[2]
+    pick = pick_ref[...]
     for c in range(3):
-        weighted = jnp.sum(rows[c * BLOCK : (c + 1) * BLOCK] * at, axis=0, keepdims=True)
-        bias.append(xyz_ref[c : c + 1, 0:SLOTS] * whole - weighted)
-    live = (ids >= 0).astype(F32)
-    bias = jnp.concatenate(bias + bias[0:1] * 5, axis=0) * (live * (-2.0 / P_SIZE))
-    pick = (iota((ATOMS_LOCAL, SLOTS), 0) == slots).astype(F32)
-    dims = (((1,), (1,)), ((), ()))
-    scattered = lax.dot_general(bias, pick, dims, precision=HIGHEST, preferred_element_type=F32)
-    out_ref[...] = pair_ref[...] + scattered[0:3]
+        part = part_ref[c * SLOTS : (c + 1) * SLOTS, :]
+        bias = jnp.sum(rows * part, axis=1, keepdims=True)
+        total = jnp.sum(bias * pick, axis=0, keepdims=True)
+        out_ref[c : c + 1, :] = pair_ref[c : c + 1, :] + total
 
 
 def device(x, z, y, core):
     return ((x * 8 + z) * 8 + y) * 2 + core
 
 
-def chip_groups():
+def chip_groups(first):
     return [
         [
-            device(x, z ^ Z_FIRST[half], y ^ Y_FIRST, half ^ middle(z ^ Z_FIRST[half]))
+            device(x, z ^ first[0], y ^ first[1], half ^ middle(z ^ first[0]))
             for z in range(8)
             for y in range(8)
         ]
@@ -251,16 +261,17 @@
 
 def first_groups():
     return [
-        [device(x, z, y ^ Y_FIRST, core ^ 1) for y in range(8) for core in range(2)]
+        [device(x, z, y ^ FIRST_FIRST, core ^ 1) for y in range(8) for core in range(2)]
         for x in range(4)
         for z in range(8)
     ]
 
 
 def second_groups():
+    first = SECOND_FIRST
     return [
         [
-            device(x ^ X_FIRST, z ^ Z_FIRST[half], y, half ^ middle(z ^ Z_FIRST[half]))
+            device(x ^ first[0], z ^ first[1], y, half ^ middle(z ^ first[1]))
             for x in range(4)
             for z in range(8)
         ]
@@ -298,7 +309,7 @@
         + [pltpu.SemaphoreType.DMA((len(inputs),))],
         compiler_params=pltpu.CompilerParams(vmem_limit_bytes=8 << 20),
     )
-    atoms = spread(sent, chip_groups())
+    atoms = spread(sent, chip_groups(ATOMS_FIRST))
     coded = [pltpu.VMEM((2, N_CHIPS, LANES), F32)]
     partial = small(dist_kernel, shaped(N_FIRST, LANES), (atoms, mine, other), coded)
     first = spread(partial, first_groups())
@@ -307,10 +318,19 @@
     biases, cv = small(
         bias_kernel, (shaped(2 * N_CHIPS, LANES), shaped(1, LANES)), (second, aux, mine, other)
     )
-    back = spread(biases, chip_groups())
-    pair = small(pair_kernel, shaped(3, ATOMS_LOCAL), (pos,))
+    back = spread(biases, chip_groups(BIAS_FIRST))
+    pair, select, part, pick = small(
+        pair_kernel,
+        (
+            shaped(3, ATOMS_LOCAL),
+            shaped(SLOTS, LANES),
+            shaped(3 * SLOTS, LANES),
+            shaped(SLOTS, ATOMS_LOCAL),
+        ),
+        (pos, aux, xyz),
+    )
     forces, cv = small(
-        force_kernel, (shaped(3, ATOMS_LOCAL), shaped(1, 2)), (back, aux, xyz, pair, cv)
+        force_kernel, (shaped(3, ATOMS_LOCAL), shaped(1, 2)), (back, select, part, pick, pair, cv)
     )
     return forces, cv.reshape(2)
 

time: 67.2 us -> 65.7 us (0.978)
  transfers between devices with their start and end apart: 3 -> 3, of which waited for: 2 -> 3; matrix products, arithmetic and copies ran while one was open for 0% -> 0% of each run, Pallas kernels for 1% -> 1%
where the time goes in v5:
time: 65.7 us; the launch traced here: 65.4 us
  starting transfers between devices  34.9 us (53%)
  blocking collectives  21.7 us (33%)
  Pallas kernels  5.01 us (8%)
  waiting for transfers between devices  3.04 us (5%)
  between operations  0.69 us (1%)
    all_to_all x2, starting transfers between devices, spread(): return lax.all_to_all(rows, ALL, 0, 0, tiled=True, axis_index_groups=groups)  32.4 us
    all_to_all x2, blocking collectives, spread(): return lax.all_to_all(rows, ALL, 0, 0, tiled=True, axis_index_groups=groups)  21.7 us
    pallas_call x6, Pallas kernels, call(): pl.pallas_call(kernel, out_shape=out_shape, out_specs=jax.tree.map(lambda...  5.01 us
    ppermute x1, starting transfers between devices, body(): other = lax.ppermute(mine, 'gz_1', [(0, 1), (1, 0)])  2.58 us
    all_to_all x2, waiting for transfers between devices, spread(): return lax.all_to_all(rows, ALL, 0, 0, tiled=True, axis_index_groups=groups)  2.18 us
  transfers between devices with their start and end apart: 3, of which 3 were waited for; matrix products, arithmetic and copies ran while one was open for 0% of the time, Pallas kernels for 1%

profile of v5, /device:TPU:1, one launch (start us, length us, event | category | flops | bytes accessed | tf_op | source)
XLA Modules:
  0.0 65.4 jit_solution(15456341933216573511)
XLA Ops:
  0.6 0.0 copy-start
  0.6 1.7 %shard_map.77 = (f32[64,128]{1,0:T(8,128)}, s32[3,128]{1,0:T(4,128)S(1)}, f32[3,128]{1,0:T(4,128)S(1)}, f32[3,512]{1,0:T(4,128)S(1)}) custom-call(s32[4,128]{1,0:T(4,128)} %bitcast.31, s32[32,128]{1,0:T(8,128)} %bitcast.30, s32[1,32]{1,0:T(1,128)} %slot_hbm.1, f32[3,512]{1,0:T(4,128)} %pos_hbm.1, s32[1,128]{1,0:T(1,128)} %bitcast.32), custom_call_target="tpu_custom_call" | custom-call | flops 2000000 | bytes 100000 | tf_op jit(solution)/shard_map/pallas_call | solution.py:64
  2.4 19.2 %all-to-all-start = ((f32[64,1,128]{2,1,0:T(1,128)}), f32[64,1,128]{2,1,0:T(1,128)S(1)}, u32[]{:S(2)}, u32[]{:S(2)}) async-start(f32[64,1,128]{2,1,0:T(1,128)} %bitcast.4), calls=%async_computation | async-start | bytes 65536 | tf_op jit(solution)/shard_map/all_to_all | solution.py:284
  21.6 0.0 copy-done
  21.6 2.6 %collective-permute-start = (f32[96,128]{1,0:T(8,128)S(1)}, f32[96,128]{1,0:T(8,128)S(1)}, u32[]{:S(2)}, u32[]{:S(2)}) collective-permute-start(f32[96,128]{1,0:T(8,128)S(1)} %bitcast.22), channel_id=1, source_target_pairs={{0,1},{1,0},{2,3},{3,2},{4,5},{5,4},{6,7},{7,6},{8,9},{9,8},{10,11... | collective-permute-start | bytes 147464 | tf_op jit(solution)/shard_map/ppermute | solution.py:289
  24.2 0.9 %collective-permute-done.other_ref = f32[96,128]{1,0:T(8,128)S(1)} collective-permute-done((f32[96,128]{1,0:T(8,128)S(1)}, f32[96,128]{1,0:T(8,128)S(1)}, u32[]{:S(2)}, u32[]{:S(2)}) %collective-permute-start) | collective-permute-done | bytes 49184 | tf_op jit(solution)/shard_map/ppermute | solution.py:289
  25.1 0.4 all-to-all-done
  25.5 0.5 shard_map.78
  26.0 9.2 %all_to_all.44 = f32[16,1,128]{2,1,0:T(1,128)S(1)} all-to-all(f32[16,1,128]{2,1,0:T(1,128)S(1)} %bitcast.28), channel_id=1, replica_groups={{9,8,11,10,13,12,15,14,1,0,3,2,5,4,7,6},{25,24,27,26,29,28,31,30,17,16,..., dimensions={0} | all-to-all | bytes 16384 | tf_op jit(solution)/shard_map/all_to_all | solution.py:284
  35.2 12.4 %all_to_all.45 = f32[32,1,128]{2,1,0:T(1,128)S(1)} all-to-all(f32[32,1,128]{2,1,0:T(1,128)S(1)} %bitcast.27), channel_id=1, replica_groups={{337,321,368,352,272,256,305,289,465,449,496,480,400,384,433,417,81,65,..., dimensions={0} | all-to-all | bytes 32768 | tf_op jit(solution)/shard_map/all_to_all | solution.py:284
  47.7 1.1 %shard_map.80 = (f32[128,128]{1,0:T(8,128)}, f32[1,128]{1,0:T(1,128)S(1)}) custom-call(f32[32,128]{1,0:T(8,128)S(1)} %bitcast.26, s32[3,128]{1,0:T(4,128)S(1)} %get-tuple-element.15.aux_ref, f32[96,128]{1,0:T(8,128)S(1)} %bitcast.24, f32[96,128]{1,0:T(8,128)S(1)} %collective-permute-done.other_ref), custom_call_target="tpu_custom_call" | custom-call | flops 2000000 | bytes 100000 | tf_op jit(solution)/shard_map/pallas_call | solution.py:64
  48.8 13.1 %all-to-all-start.3 = ((f32[64,2,128]{2,1,0:T(2,128)}), f32[64,2,128]{2,1,0:T(2,128)S(1)}, u32[]{:S(2)}, u32[]{:S(2)}) async-start(f32[64,2,128]{2,1,0:T(2,128)} %bitcast.15), calls=%async_computation.3 | async-start | bytes 131072 | tf_op jit(solution)/shard_map/all_to_all | solution.py:284
  61.9 0.9 %shard_map.81 = (f32[3,512]{1,0:T(4,128)S(1)}, f32[32,128]{1,0:T(8,128)S(1)}, f32[96,128]{1,0:T(8,128)S(1)}, f32[32,512]{1,0:T(8,128)S(1)}) custom-call(f32[3,512]{1,0:T(4,128)S(1)} %get-tuple-element.17.pos_ref, s32[3,128]{1,0:T(4,128)S(1)} %get-tuple-element.15.aux_ref, f32[3,128]{1,0:T(4,128)S(1)} %get-tuple-element.18.xyz_ref), custom_call_target="tpu_custom_call" | custom-call | flops 2000000 | bytes 100000 | tf_op jit(solution)/shard_map/pallas_call | solution.py:64
  62.8 1.7 %all-to-all-done.3 = f32[64,2,128]{2,1,0:T(2,128)S(1)} async-done(((f32[64,2,128]{2,1,0:T(2,128)}), f32[64,2,128]{2,1,0:T(2,128)S(1)}, u32[]{:S(2)}, u32[]{:S(2)}) %all-to-all-start.3) | async-done | bytes 65568 | tf_op jit(solution)/shard_map/all_to_all | solution.py:284
  64.5 0.9 %shard_map.82 = (f32[3,512]{1,0:T(4,128)}, f32[1,2]{1,0:T(1,128)}) custom-call(f32[128,128]{1,0:T(8,128)S(1)} %bitcast.21, f32[32,128]{1,0:T(8,128)S(1)} %get-tuple-element.19.select_ref, f32[96,128]{1,0:T(8,128)S(1)} %get-tuple-element.20.part_ref, f32[32,512]{1,0:T(8,128)S(1)} %get-tuple-element.21.pick_ref, f32[3,512]{1,0:T(4,128)S(1)} %get-tuple-element.22.pair_ref, ...), custom_call_target="tpu_custom_call" | custom-call | flops 2000000 | bytes 100000 | tf_op jit(solution)/shard_map/pallas_call | solution.py:64
  (1 shorter events, 0.0 us)
Async XLA Ops:
  0.6 21.0 %copy-start = (f32[128,3,32]{0,2,1:T(8,128)S(1)}, f32[128,3,32]{0,2,1:T(8,128)}, u32[]{:S(2)}) copy-start(f32[128,3,32]{0,2,1:T(8,128)} %param.7) | copy-start | bytes 147460
  2.4 23.1 %all-to-all-start = ((f32[64,1,128]{2,1,0:T(1,128)}), f32[64,1,128]{2,1,0:T(1,128)S(1)}, u32[]{:S(2)}, u32[]{:S(2)}) async-start(f32[64,1,128]{2,1,0:T(1,128)} %bitcast.4), calls=%async_computation | async-start | bytes 65536 | tf_op jit(solution)/shard_map/all_to_all | solution.py:284
  21.6 3.5 %collective-permute-start = (f32[96,128]{1,0:T(8,128)S(1)}, f32[96,128]{1,0:T(8,128)S(1)}, u32[]{:S(2)}, u32[]{:S(2)}) collective-permute-start(f32[96,128]{1,0:T(8,128)S(1)} %bitcast.22), channel_id=1, source_target_pairs={{0,1},{1,0},{2,3},{3,2},{4,5},{5,4},{6,7},{7,6},{8,9},{9,8},{10,11... | collective-permute-start | bytes 147464 | tf_op jit(solution)/shard_map/ppermute | solution.py:289
  48.8 15.8 %all-to-all-start.3 = ((f32[64,2,128]{2,1,0:T(2,128)}), f32[64,2,128]{2,1,0:T(2,128)S(1)}, u32[]{:S(2)}, u32[]{:S(2)}) async-start(f32[64,2,128]{2,1,0:T(2,128)} %bitcast.15), calls=%async_computation.3 | async-start | bytes 131072 | tf_op jit(solution)/shard_map/all_to_all | solution.py:284

commit v6 on v5

--- a/solution.py
+++ b/solution.py
@@ -149,13 +149,12 @@
     shift = offset - row * LANES
     first = order_ref[pl.ds(row, 1), :]
     second = order_ref[pl.ds(jnp.minimum(row + 1, P_SIZE // LANES - 1), 1), :]
+    entries = jnp.where(lane >= shift, first, second)
     ids = jnp.full((1, LANES), -1, I32)
     for part in range(4):
         start = shift - part * SLOTS
         turn = jnp.where(start <= 0, -start, LANES - start)
-        here_first = k < LANES - shift
-        turned = jnp.where(here_first, pltpu.roll(first, turn, 1), pltpu.roll(second, turn, 1))
-        ids = jnp.where(live & (lane // SLOTS == part), turned, ids)
+        ids = jnp.where(live & (lane // SLOTS == part), pltpu.roll(entries, turn, 1), ids)
     xyz_ref[...] = xyz
     part = lane // SLOTS
     row_out = jnp.where(part == 0, xyz[0:1], jnp.where(part == 1, xyz[1:2], xyz[2:3]))
@@ -280,6 +279,19 @@
     ]
 
 
+def apart(a, b, size):
+    return min((a - b) % size, (b - a) % size)
+
+
+def far_first(groups):
+    def hops(a, b):
+        a, b = a // 2, b // 2
+        x, z, y = (a // 64, b // 64, 4), (a // 8 % 8, b // 8 % 8, 8), (a % 8, b % 8, 8)
+        return apart(*x) + apart(*z) + apart(*y)
+
+    return [[g[0]] + sorted(g[1:], key=lambda d: -hops(d, g[0])) for g in groups]
+
+
 def spread(rows, groups):
     return lax.all_to_all(rows, ALL, 0, 0, tiled=True, axis_index_groups=groups)
 
@@ -309,12 +321,12 @@
         + [pltpu.SemaphoreType.DMA((len(inputs),))],
         compiler_params=pltpu.CompilerParams(vmem_limit_bytes=8 << 20),
     )
-    atoms = spread(sent, chip_groups(ATOMS_FIRST))
+    atoms = spread(sent, far_first(chip_groups(ATOMS_FIRST)))
     coded = [pltpu.VMEM((2, N_CHIPS, LANES), F32)]
     partial = small(dist_kernel, shaped(N_FIRST, LANES), (atoms, mine, other), coded)
-    first = spread(partial, first_groups())
+    first = spread(partial, far_first(first_groups()))
     row_sum = small(sum_kernel, shaped(N_SECOND, LANES), (first,))
-    second = spread(row_sum, second_groups())
+    second = spread(row_sum, far_first(second_groups()))
     biases, cv = small(
         bias_kernel, (shaped(2 * N_CHIPS, LANES), shaped(1, LANES)), (second, aux, mine, other)
     )

time: 65.7 us -> 65.8 us (level)
  no operation moved by 1% of the time
where the time goes in v6:
time: 65.8 us; the launch traced here: 65.5 us
  starting transfers between devices  34.9 us (53%)
  blocking collectives  21.5 us (33%)
  Pallas kernels  5.01 us (8%)
  waiting for transfers between devices  3.46 us (5%)
  between operations  0.69 us (1%)
    all_to_all x2, starting transfers between devices, spread(): return lax.all_to_all(rows, ALL, 0, 0, tiled=True, axis_index_groups=groups)  32.3 us
    all_to_all x2, blocking collectives, spread(): return lax.all_to_all(rows, ALL, 0, 0, tiled=True, axis_index_groups=groups)  21.5 us
    pallas_call x6, Pallas kernels, call(): pl.pallas_call(kernel, out_shape=out_shape, out_specs=jax.tree.map(lambda...  5.01 us
    all_to_all x2, waiting for transfers between devices, spread(): return lax.all_to_all(rows, ALL, 0, 0, tiled=True, axis_index_groups=groups)  2.6 us
    ppermute x1, starting transfers between devices, body(): other = lax.ppermute(mine, 'gz_1', [(0, 1), (1, 0)])  2.58 us
  transfers between devices with their start and end apart: 3, of which 3 were waited for; matrix products, arithmetic and copies ran while one was open for 0% of the time, Pallas kernels for 1%

profile of v6, /device:TPU:1, one launch (start us, length us, event | category | flops | bytes accessed | tf_op | source)
XLA Modules:
  0.0 65.5 jit_solution(6154842026475316734)
XLA Ops:
  0.6 0.0 copy-start
  0.6 1.7 %shard_map.77 = (f32[64,128]{1,0:T(8,128)}, s32[3,128]{1,0:T(4,128)S(1)}, f32[3,128]{1,0:T(4,128)S(1)}, f32[3,512]{1,0:T(4,128)S(1)}) custom-call(s32[4,128]{1,0:T(4,128)} %bitcast.31, s32[32,128]{1,0:T(8,128)} %bitcast.30, s32[1,32]{1,0:T(1,128)} %slot_hbm.1, f32[3,512]{1,0:T(4,128)} %pos_hbm.1, s32[1,128]{1,0:T(1,128)} %bitcast.32), custom_call_target="tpu_custom_call" | custom-call | flops 2000000 | bytes 100000 | tf_op jit(solution)/shard_map/pallas_call | solution.py:64
  2.4 19.0 %all-to-all-start = ((f32[64,1,128]{2,1,0:T(1,128)}), f32[64,1,128]{2,1,0:T(1,128)S(1)}, u32[]{:S(2)}, u32[]{:S(2)}) async-start(f32[64,1,128]{2,1,0:T(1,128)} %bitcast.4), calls=%async_computation | async-start | bytes 65536 | tf_op jit(solution)/shard_map/all_to_all | solution.py:296
  21.4 0.0 copy-done
  21.4 2.6 %collective-permute-start = (f32[96,128]{1,0:T(8,128)S(1)}, f32[96,128]{1,0:T(8,128)S(1)}, u32[]{:S(2)}, u32[]{:S(2)}) collective-permute-start(f32[96,128]{1,0:T(8,128)S(1)} %bitcast.22), channel_id=1, source_target_pairs={{0,1},{1,0},{2,3},{3,2},{4,5},{5,4},{6,7},{7,6},{8,9},{9,8},{10,11... | collective-permute-start | bytes 147464 | tf_op jit(solution)/shard_map/ppermute | solution.py:301
  24.0 0.9 %collective-permute-done.other_ref = f32[96,128]{1,0:T(8,128)S(1)} collective-permute-done((f32[96,128]{1,0:T(8,128)S(1)}, f32[96,128]{1,0:T(8,128)S(1)}, u32[]{:S(2)}, u32[]{:S(2)}) %collective-permute-start) | collective-permute-done | bytes 49184 | tf_op jit(solution)/shard_map/ppermute | solution.py:301
  24.9 0.5 all-to-all-done
  25.4 0.5 shard_map.78
  25.9 9.2 %all_to_all.44 = f32[16,1,128]{2,1,0:T(1,128)S(1)} all-to-all(f32[16,1,128]{2,1,0:T(1,128)S(1)} %bitcast.28), channel_id=1, replica_groups={{9,1,0,15,14,3,2,13,12,5,4,11,10,7,6,8},{25,17,16,31,30,19,18,29,28,21,..., dimensions={0} | all-to-all | bytes 16384 | tf_op jit(solution)/shard_map/all_to_all | solution.py:296
  35.2 12.2 %all_to_all.45 = f32[32,1,128]{2,1,0:T(1,128)S(1)} all-to-all(f32[32,1,128]{2,1,0:T(1,128)S(1)} %bitcast.27), channel_id=1, replica_groups={{337,16,400,0,33,144,272,384,417,112,49,128,161,256,289,496,433,65,96,2..., dimensions={0} | all-to-all | bytes 32768 | tf_op jit(solution)/shard_map/all_to_all | solution.py:296
  47.4 1.1 %shard_map.80 = (f32[128,128]{1,0:T(8,128)}, f32[1,128]{1,0:T(1,128)S(1)}) custom-call(f32[32,128]{1,0:T(8,128)S(1)} %bitcast.26, s32[3,128]{1,0:T(4,128)S(1)} %get-tuple-element.15.aux_ref, f32[96,128]{1,0:T(8,128)S(1)} %bitcast.24, f32[96,128]{1,0:T(8,128)S(1)} %collective-permute-done.other_ref), custom_call_target="tpu_custom_call" | custom-call | flops 2000000 | bytes 100000 | tf_op jit(solution)/shard_map/pallas_call | solution.py:64
  48.5 13.2 %all-to-all-start.3 = ((f32[64,2,128]{2,1,0:T(2,128)}), f32[64,2,128]{2,1,0:T(2,128)S(1)}, u32[]{:S(2)}, u32[]{:S(2)}) async-start(f32[64,2,128]{2,1,0:T(2,128)} %bitcast.15), calls=%async_computation.3 | async-start | bytes 131072 | tf_op jit(solution)/shard_map/all_to_all | solution.py:296
  61.7 0.9 %shard_map.81 = (f32[3,512]{1,0:T(4,128)S(1)}, f32[32,128]{1,0:T(8,128)S(1)}, f32[96,128]{1,0:T(8,128)S(1)}, f32[32,512]{1,0:T(8,128)S(1)}) custom-call(f32[3,512]{1,0:T(4,128)S(1)} %get-tuple-element.17.pos_ref, s32[3,128]{1,0:T(4,128)S(1)} %get-tuple-element.15.aux_ref, f32[3,128]{1,0:T(4,128)S(1)} %get-tuple-element.18.xyz_ref), custom_call_target="tpu_custom_call" | custom-call | flops 2000000 | bytes 100000 | tf_op jit(solution)/shard_map/pallas_call | solution.py:64
  62.6 2.1 %all-to-all-done.3 = f32[64,2,128]{2,1,0:T(2,128)S(1)} async-done(((f32[64,2,128]{2,1,0:T(2,128)}), f32[64,2,128]{2,1,0:T(2,128)S(1)}, u32[]{:S(2)}, u32[]{:S(2)}) %all-to-all-start.3) | async-done | bytes 65568 | tf_op jit(solution)/shard_map/all_to_all | solution.py:296
  64.6 0.9 %shard_map.82 = (f32[3,512]{1,0:T(4,128)}, f32[1,2]{1,0:T(1,128)}) custom-call(f32[128,128]{1,0:T(8,128)S(1)} %bitcast.21, f32[32,128]{1,0:T(8,128)S(1)} %get-tuple-element.19.select_ref, f32[96,128]{1,0:T(8,128)S(1)} %get-tuple-element.20.part_ref, f32[32,512]{1,0:T(8,128)S(1)} %get-tuple-element.21.pick_ref, f32[3,512]{1,0:T(4,128)S(1)} %get-tuple-element.22.pair_ref, ...), custom_call_target="tpu_custom_call" | custom-call | flops 2000000 | bytes 100000 | tf_op jit(solution)/shard_map/pallas_call | solution.py:64
  (1 shorter events, 0.0 us)
Async XLA Ops:
  0.6 20.8 %copy-start = (f32[128,3,32]{0,2,1:T(8,128)S(1)}, f32[128,3,32]{0,2,1:T(8,128)}, u32[]{:S(2)}) copy-start(f32[128,3,32]{0,2,1:T(8,128)} %param.7) | copy-start | bytes 147460
  2.4 23.1 %all-to-all-start = ((f32[64,1,128]{2,1,0:T(1,128)}), f32[64,1,128]{2,1,0:T(1,128)S(1)}, u32[]{:S(2)}, u32[]{:S(2)}) async-start(f32[64,1,128]{2,1,0:T(1,128)} %bitcast.4), calls=%async_computation | async-start | bytes 65536 | tf_op jit(solution)/shard_map/all_to_all | solution.py:296
  21.4 3.5 %collective-permute-start = (f32[96,128]{1,0:T(8,128)S(1)}, f32[96,128]{1,0:T(8,128)S(1)}, u32[]{:S(2)}, u32[]{:S(2)}) collective-permute-start(f32[96,128]{1,0:T(8,128)S(1)} %bitcast.22), channel_id=1, source_target_pairs={{0,1},{1,0},{2,3},{3,2},{4,5},{5,4},{6,7},{7,6},{8,9},{9,8},{10,11... | collective-permute-start | bytes 147464 | tf_op jit(solution)/shard_map/ppermute | solution.py:301
  48.5 16.2 %all-to-all-start.3 = ((f32[64,2,128]{2,1,0:T(2,128)}), f32[64,2,128]{2,1,0:T(2,128)S(1)}, u32[]{:S(2)}, u32[]{:S(2)}) async-start(f32[64,2,128]{2,1,0:T(2,128)} %bitcast.15), calls=%async_computation.3 | async-start | bytes 131072 | tf_op jit(solution)/shard_map/all_to_all | solution.py:296

commit v7 on v5

--- a/solution.py
+++ b/solution.py
@@ -149,13 +149,12 @@
     shift = offset - row * LANES
     first = order_ref[pl.ds(row, 1), :]
     second = order_ref[pl.ds(jnp.minimum(row + 1, P_SIZE // LANES - 1), 1), :]
+    entries = jnp.where(lane >= shift, first, second)
     ids = jnp.full((1, LANES), -1, I32)
     for part in range(4):
         start = shift - part * SLOTS
         turn = jnp.where(start <= 0, -start, LANES - start)
-        here_first = k < LANES - shift
-        turned = jnp.where(here_first, pltpu.roll(first, turn, 1), pltpu.roll(second, turn, 1))
-        ids = jnp.where(live & (lane // SLOTS == part), turned, ids)
+        ids = jnp.where(live & (lane // SLOTS == part), pltpu.roll(entries, turn, 1), ids)
     xyz_ref[...] = xyz
     part = lane // SLOTS
     row_out = jnp.where(part == 0, xyz[0:1], jnp.where(part == 1, xyz[1:2], xyz[2:3]))

time: 65.7 us -> 65.7 us (level)
  no operation moved by 1% of the time
where the time goes in v7:
time: 65.7 us; the launch traced here: 65.4 us
  starting transfers between devices  34.9 us (53%)
  blocking collectives  21.7 us (33%)
  Pallas kernels  5.01 us (8%)
  waiting for transfers between devices  3.04 us (5%)
  between operations  0.69 us (1%)
    all_to_all x2, starting transfers between devices, spread(): return lax.all_to_all(rows, ALL, 0, 0, tiled=True, axis_index_groups=groups)  32.4 us
    all_to_all x2, blocking collectives, spread(): return lax.all_to_all(rows, ALL, 0, 0, tiled=True, axis_index_groups=groups)  21.7 us
    pallas_call x6, Pallas kernels, call(): pl.pallas_call(kernel, out_shape=out_shape, out_specs=jax.tree.map(lambda...  5.01 us
    ppermute x1, starting transfers between devices, body(): other = lax.ppermute(mine, 'gz_1', [(0, 1), (1, 0)])  2.58 us
    all_to_all x2, waiting for transfers between devices, spread(): return lax.all_to_all(rows, ALL, 0, 0, tiled=True, axis_index_groups=groups)  2.18 us
  transfers between devices with their start and end apart: 3, of which 3 were waited for; matrix products, arithmetic and copies ran while one was open for 0% of the time, Pallas kernels for 1%

profile of v7, /device:TPU:1, one launch (start us, length us, event | category | flops | bytes accessed | tf_op | source)
XLA Modules:
  0.0 65.4 jit_solution(9661267772499361907)
XLA Ops:
  0.6 0.0 copy-start
  0.6 1.7 %shard_map.77 = (f32[64,128]{1,0:T(8,128)}, s32[3,128]{1,0:T(4,128)S(1)}, f32[3,128]{1,0:T(4,128)S(1)}, f32[3,512]{1,0:T(4,128)S(1)}) custom-call(s32[4,128]{1,0:T(4,128)} %bitcast.31, s32[32,128]{1,0:T(8,128)} %bitcast.30, s32[1,32]{1,0:T(1,128)} %slot_hbm.1, f32[3,512]{1,0:T(4,128)} %pos_hbm.1, s32[1,128]{1,0:T(1,128)} %bitcast.32), custom_call_target="tpu_custom_call" | custom-call | flops 2000000 | bytes 100000 | tf_op jit(solution)/shard_map/pallas_call | solution.py:64
  2.4 19.2 %all-to-all-start = ((f32[64,1,128]{2,1,0:T(1,128)}), f32[64,1,128]{2,1,0:T(1,128)S(1)}, u32[]{:S(2)}, u32[]{:S(2)}) async-start(f32[64,1,128]{2,1,0:T(1,128)} %bitcast.4), calls=%async_computation | async-start | bytes 65536 | tf_op jit(solution)/shard_map/all_to_all | solution.py:283
  21.6 0.0 copy-done
  21.6 2.6 %collective-permute-start = (f32[96,128]{1,0:T(8,128)S(1)}, f32[96,128]{1,0:T(8,128)S(1)}, u32[]{:S(2)}, u32[]{:S(2)}) collective-permute-start(f32[96,128]{1,0:T(8,128)S(1)} %bitcast.22), channel_id=1, source_target_pairs={{0,1},{1,0},{2,3},{3,2},{4,5},{5,4},{6,7},{7,6},{8,9},{9,8},{10,11... | collective-permute-start | bytes 147464 | tf_op jit(solution)/shard_map/ppermute | solution.py:288
  24.2 0.9 %collective-permute-done.other_ref = f32[96,128]{1,0:T(8,128)S(1)} collective-permute-done((f32[96,128]{1,0:T(8,128)S(1)}, f32[96,128]{1,0:T(8,128)S(1)}, u32[]{:S(2)}, u32[]{:S(2)}) %collective-permute-start) | collective-permute-done | bytes 49184 | tf_op jit(solution)/shard_map/ppermute | solution.py:288
  25.1 0.4 all-to-all-done
  25.5 0.5 shard_map.78
  26.0 9.2 %all_to_all.44 = f32[16,1,128]{2,1,0:T(1,128)S(1)} all-to-all(f32[16,1,128]{2,1,0:T(1,128)S(1)} %bitcast.28), channel_id=1, replica_groups={{9,8,11,10,13,12,15,14,1,0,3,2,5,4,7,6},{25,24,27,26,29,28,31,30,17,16,..., dimensions={0} | all-to-all | bytes 16384 | tf_op jit(solution)/shard_map/all_to_all | solution.py:283
  35.2 12.4 %all_to_all.45 = f32[32,1,128]{2,1,0:T(1,128)S(1)} all-to-all(f32[32,1,128]{2,1,0:T(1,128)S(1)} %bitcast.27), channel_id=1, replica_groups={{337,321,368,352,272,256,305,289,465,449,496,480,400,384,433,417,81,65,..., dimensions={0} | all-to-all | bytes 32768 | tf_op jit(solution)/shard_map/all_to_all | solution.py:283
  47.7 1.1 %shard_map.80 = (f32[128,128]{1,0:T(8,128)}, f32[1,128]{1,0:T(1,128)S(1)}) custom-call(f32[32,128]{1,0:T(8,128)S(1)} %bitcast.26, s32[3,128]{1,0:T(4,128)S(1)} %get-tuple-element.15.aux_ref, f32[96,128]{1,0:T(8,128)S(1)} %bitcast.24, f32[96,128]{1,0:T(8,128)S(1)} %collective-permute-done.other_ref), custom_call_target="tpu_custom_call" | custom-call | flops 2000000 | bytes 100000 | tf_op jit(solution)/shard_map/pallas_call | solution.py:64
  48.8 13.1 %all-to-all-start.3 = ((f32[64,2,128]{2,1,0:T(2,128)}), f32[64,2,128]{2,1,0:T(2,128)S(1)}, u32[]{:S(2)}, u32[]{:S(2)}) async-start(f32[64,2,128]{2,1,0:T(2,128)} %bitcast.15), calls=%async_computation.3 | async-start | bytes 131072 | tf_op jit(solution)/shard_map/all_to_all | solution.py:283
  61.9 0.9 %shard_map.81 = (f32[3,512]{1,0:T(4,128)S(1)}, f32[32,128]{1,0:T(8,128)S(1)}, f32[96,128]{1,0:T(8,128)S(1)}, f32[32,512]{1,0:T(8,128)S(1)}) custom-call(f32[3,512]{1,0:T(4,128)S(1)} %get-tuple-element.17.pos_ref, s32[3,128]{1,0:T(4,128)S(1)} %get-tuple-element.15.aux_ref, f32[3,128]{1,0:T(4,128)S(1)} %get-tuple-element.18.xyz_ref), custom_call_target="tpu_custom_call" | custom-call | flops 2000000 | bytes 100000 | tf_op jit(solution)/shard_map/pallas_call | solution.py:64
  62.8 1.7 %all-to-all-done.3 = f32[64,2,128]{2,1,0:T(2,128)S(1)} async-done(((f32[64,2,128]{2,1,0:T(2,128)}), f32[64,2,128]{2,1,0:T(2,128)S(1)}, u32[]{:S(2)}, u32[]{:S(2)}) %all-to-all-start.3) | async-done | bytes 65568 | tf_op jit(solution)/shard_map/all_to_all | solution.py:283
  64.5 0.9 %shard_map.82 = (f32[3,512]{1,0:T(4,128)}, f32[1,2]{1,0:T(1,128)}) custom-call(f32[128,128]{1,0:T(8,128)S(1)} %bitcast.21, f32[32,128]{1,0:T(8,128)S(1)} %get-tuple-element.19.select_ref, f32[96,128]{1,0:T(8,128)S(1)} %get-tuple-element.20.part_ref, f32[32,512]{1,0:T(8,128)S(1)} %get-tuple-element.21.pick_ref, f32[3,512]{1,0:T(4,128)S(1)} %get-tuple-element.22.pair_ref, ...), custom_call_target="tpu_custom_call" | custom-call | flops 2000000 | bytes 100000 | tf_op jit(solution)/shard_map/pallas_call | solution.py:64
  (1 shorter events, 0.0 us)
Async XLA Ops:
  0.6 21.0 %copy-start = (f32[128,3,32]{0,2,1:T(8,128)S(1)}, f32[128,3,32]{0,2,1:T(8,128)}, u32[]{:S(2)}) copy-start(f32[128,3,32]{0,2,1:T(8,128)} %param.7) | copy-start | bytes 147460
  2.4 23.1 %all-to-all-start = ((f32[64,1,128]{2,1,0:T(1,128)}), f32[64,1,128]{2,1,0:T(1,128)S(1)}, u32[]{:S(2)}, u32[]{:S(2)}) async-start(f32[64,1,128]{2,1,0:T(1,128)} %bitcast.4), calls=%async_computation | async-start | bytes 65536 | tf_op jit(solution)/shard_map/all_to_all | solution.py:283
  21.6 3.5 %collective-permute-start = (f32[96,128]{1,0:T(8,128)S(1)}, f32[96,128]{1,0:T(8,128)S(1)}, u32[]{:S(2)}, u32[]{:S(2)}) collective-permute-start(f32[96,128]{1,0:T(8,128)S(1)} %bitcast.22), channel_id=1, source_target_pairs={{0,1},{1,0},{2,3},{3,2},{4,5},{5,4},{6,7},{7,6},{8,9},{9,8},{10,11... | collective-permute-start | bytes 147464 | tf_op jit(solution)/shard_map/ppermute | solution.py:288
  48.8 15.8 %all-to-all-start.3 = ((f32[64,2,128]{2,1,0:T(2,128)}), f32[64,2,128]{2,1,0:T(2,128)S(1)}, u32[]{:S(2)}, u32[]{:S(2)}) async-start(f32[64,2,128]{2,1,0:T(2,128)} %bitcast.15), calls=%async_computation.3 | async-start | bytes 131072 | tf_op jit(solution)/shard_map/all_to_all | solution.py:283
